TPU v7x, 32 devices: a whole 2x2x4 slice. The times are simulated.
32 devices in a mesh: prow: 4 (over y, core), pcol: 8 (over z, x).
Axes of the slice: x: 2, y: 2, z: 4, core: 2. Of those that a mesh axis runs over, the one named last changes fastest.
Arguments:
- inverse_cov: bfloat16 [8192, 8192], P('prow', 'pcol'), may hold values from -0.5 to 4.5, as said below
- cosines: float32 [8192, 8192], P('prow', 'pcol'), may hold values from -1 to 1, as said below
- sky_maps: bfloat16 [8192, 192], P('pcol'), may hold values from -6 to 6
Outputs:
- filtered: bfloat16 [8192, 192], P('prow')
- spectra: float32 [64, 192], replicated
Inputs may be any that keep to these rules, and one draw needn't show every extreme that they name: `inverse_cov`: symmetric, with a dominant diagonal. `cosines`: symmetric.
All inputs are finite; a program needn't handle non-finite values.
Results may differ from a plain program's by a relative error of at most 0.0033.
Values may be sent and summed in bfloat16 or wider, within the bound.
A program may use at most 128 MiB of HBM per device.

v0:
```python
import functools
import math
import random

import jax
import jax.numpy as jnp
import numpy as np
from jax import lax
from jax.experimental import pallas as pl
from jax.experimental.pallas import tpu as pltpu
from jax.sharding import PartitionSpec as P

L = 64
LMIN = 2
TILE = 256
STRIP = 16
GROUP = 11
CHUNKS = 6
LEVELS = GROUP * CHUNKS


def transform_matrix(npix, devices):
    top = LMIN + L - 1
    each = -(-L // devices)
    a = [math.comb(2 * k, k) / 4.0**k for k in range(top + 1)]
    out = np.zeros((devices * each, LEVELS))
    for l in range(LMIN, top + 1):
        owner, place = divmod(l - LMIN, each)
        row = out[owner * each + place]
        for k in range(l + 1):
            row[abs(l - 2 * k)] += a[k] * a[l - k]
        row *= (2 * l + 1) / npix
    return out.astype(np.float32), each


def pair_up(tiles, n):
    items = []
    for col in range(n):
        mine = sorted((t for t in tiles if t[1] == col), key=lambda t: t[0])
        for k in range(0, len(mine), 2):
            first = mine[k]
            second = mine[k + 1] if k + 1 < len(mine) else (first[0], col, 0)
            items.append((first[0], second[0], first[2], second[2], col))
    return items


def work_tables(n):
    lower = [[(h * n + i, j, 2) for i in range(n) for j in range(n)] for h in range(2)]
    rng = random.Random(0)
    best = None
    for _ in range(20000):
        sets = []
        cross = [[rng.random() < 0.5 for _ in range(n)] for _ in range(n)]
        for h in range(2):
            tiles = []
            for i in range(n):
                tiles.append((h * n + i, i, 1))
                for j in range(i):
                    a, b = (i, j) if rng.random() < 0.5 else (j, i)
                    tiles.append((h * n + a, b, 2))
                for j in range(n):
                    if h == 0 and cross[i][j]:
                        tiles.append((n + i, j, 2))
                    if h == 1 and not cross[i][j]:
                        tiles.append((j, i, 2))
            sets.append(pair_up(tiles, n))
        cost = max(len(s) for s in sets)
        if best is None or cost < best[0]:
            best = (cost, sets)
        if 2 * cost <= n * n + n // 2 + 1:
            break
    kinds = [pair_up(lower[0], n), pair_up(lower[1], n), pair_up(lower[1], n), pair_up(lower[0], n)] + best[1]
    longest = max(len(k) for k in kinds)
    table = np.zeros((len(kinds), longest + 1, 5), np.int32)
    for k, items in enumerate(kinds):
        table[k, : len(items)] = items
    counts = np.array([len(k) for k in kinds], np.int32)
    return table.reshape(-1), counts, longest + 1


def moments_kernel(
    stride, table, counts, cos_hbm, ft, fct, out,
    xbuf, x2, prev, cur, buf_a, buf_b, lhs, fj, acc, sem,
):
    r = lax.axis_index("prow")
    c = lax.axis_index("pcol")
    q, h = c // 2, c % 2
    kind = jnp.where(r > q, h, jnp.where(r < q, 2 + h, 4 + h))
    n_items = counts[kind]

    def field(item, f):
        return table[(kind * stride + item) * 5 + f]

    def tile_copy(item, half):
        row = pl.multiple_of(field(item, half) * TILE, TILE)
        col = pl.multiple_of(field(item, 4) * TILE, TILE)
        return pltpu.make_async_copy(
            cos_hbm.at[pl.ds(row, TILE), pl.ds(col, TILE)],
            xbuf.at[pl.ds(half * TILE, TILE)],
            sem.at[half],
        )

    def fetch(item):
        tile_copy(item, 0).start()
        tile_copy(item, 1).start()

    def begin(item):
        tile_copy(item, 0).wait()
        tile_copy(item, 1).wait()
        x = xbuf[...]
        x2[...] = x + x
        prev[...] = (x + x) * x - 1.0
        cur[...] = x

    def set_operands(item):
        col = pl.multiple_of(field(item, 4) * TILE, TILE)
        for half in range(2):
            row = pl.multiple_of(field(item, half) * TILE, TILE)
            weight = field(item, 2 + half).astype(jnp.float32)
            value = ft[:, pl.ds(row, TILE)].astype(jnp.float32) * weight
            lhs[:, half * TILE : (half + 1) * TILE] = value.astype(jnp.bfloat16)
        fj[...] = fct[:, pl.ds(col, TILE)].astype(jnp.float32)

    n_strips = 2 * TILE // STRIP

    def gen_strip(buf, s):
        rows = pl.ds(s * STRIP, STRIP)
        xx = x2[rows, :]
        p = prev[rows, :]
        t = cur[rows, :]
        for g in range(GROUP):
            p, t = t, xx * t - p
            buf[g, rows, :] = t.astype(jnp.bfloat16)
        prev[rows, :] = p
        cur[rows, :] = t

    def half_step(gen, use, level0):
        done = 0
        for g in range(GROUP):
            upto = (g + 1) * n_strips // GROUP
            for s in range(done, upto):
                gen_strip(gen, s)
            done = upto
            image = jnp.dot(lhs[...], use[g], preferred_element_type=jnp.float32)
            prod = image * fj[...]
            half_tile = TILE // 2
            acc[level0 + g] += prod[:, :half_tile] + prod[:, half_tile:]

    acc[...] = jnp.zeros_like(acc)
    fetch(0)
    begin(0)
    for s in range(n_strips):
        gen_strip(buf_a, s)

    def item_loop(item, carry):
        fetch(item + 1)
        set_operands(item)

        def chunk_loop(cp, carry):
            half_step(buf_b, buf_a, cp * 2 * GROUP)

            @pl.when(cp == CHUNKS // 2 - 1)
            def _():
                begin(item + 1)

            half_step(buf_a, buf_b, cp * 2 * GROUP + GROUP)
            return carry

        return lax.fori_loop(0, CHUNKS // 2, chunk_loop, carry)

    lax.fori_loop(0, n_items, item_loop, 0)
    out[...] = jnp.sum(acc[...], axis=-1)


def spectra_moments(cosines, ft, fct):
    maps = ft.shape[0]
    n = cosines.shape[1] // TILE
    table, counts, stride = work_tables(n)
    vmem = pl.BlockSpec(memory_space=pltpu.VMEM)
    smem = pl.BlockSpec(memory_space=pltpu.SMEM)
    return pl.pallas_call(
        functools.partial(moments_kernel, stride),
        out_shape=jax.ShapeDtypeStruct((LEVELS, maps), jnp.float32),
        in_specs=[smem, smem, pl.BlockSpec(memory_space=pl.ANY), vmem, vmem],
        out_specs=vmem,
        scratch_shapes=[
            pltpu.VMEM((2 * TILE, TILE), jnp.float32),
            pltpu.VMEM((2 * TILE, TILE), jnp.float32),
            pltpu.VMEM((2 * TILE, TILE), jnp.float32),
            pltpu.VMEM((2 * TILE, TILE), jnp.float32),
            pltpu.VMEM((GROUP, 2 * TILE, TILE), jnp.bfloat16),
            pltpu.VMEM((GROUP, 2 * TILE, TILE), jnp.bfloat16),
            pltpu.VMEM((maps, 2 * TILE), jnp.bfloat16),
            pltpu.VMEM((maps, TILE), jnp.float32),
            pltpu.VMEM((LEVELS, maps, TILE // 2), jnp.float32),
            pltpu.SemaphoreType.DMA((2,)),
        ],
        compiler_params=pltpu.CompilerParams(vmem_limit_bytes=48 * 2**20),
        name="moments",
    )(jnp.asarray(table), jnp.asarray(counts), cosines, ft, fct)


MESH = pl.DeviceIdType.MESH


def spread_kernel(n_q, block, out, far_send, near_send, far_recv, side_send, side_recv):
    r = lax.axis_index("prow")
    c = lax.axis_index("pcol")
    q, h = c // 2, c % 2
    width = block.shape[1]
    pieces = far_recv.shape[0]
    step = width // pieces
    partner = (r, c + 1 - 2 * h)
    above, below = (r, c + 2), (r, c - 2)
    has_above, has_below = q < n_q - 1, q > 0
    barrier = pltpu.get_barrier_semaphore()
    pl.semaphore_signal(barrier, inc=1, device_id=partner, device_id_type=MESH)

    @pl.when(has_above)
    def _():
        pl.semaphore_signal(barrier, inc=1, device_id=above, device_id_type=MESH)

    @pl.when(has_below)
    def _():
        pl.semaphore_signal(barrier, inc=1, device_id=below, device_id_type=MESH)

    pl.semaphore_wait(barrier, 1 + has_above.astype(jnp.int32) + has_below.astype(jnp.int32))

    source = q == r
    up = jnp.logical_and(q >= r, has_above)
    down = jnp.logical_and(q <= r, has_below)

    def columns(half, k):
        return pl.ds(pl.multiple_of(half * width + k * step, 128), step)

    def remote(src, k, send, recv, device):
        return pltpu.make_async_remote_copy(
            src_ref=src,
            dst_ref=out.at[:, columns(h, k)],
            send_sem=send.at[k],
            recv_sem=recv.at[k],
            device_id=device,
            device_id_type=MESH,
        )

    def send_all(src, k):
        @pl.when(up)
        def _():
            remote(src, k, far_send, far_recv, above).start()

        @pl.when(down)
        def _():
            remote(src, k, near_send, far_recv, below).start()

        remote(src, k, side_send, side_recv, partner).start()

    @pl.when(source)
    def _():
        for k in range(pieces):
            send_all(block.at[:, pl.ds(k * step, step)], k)
        out[:, pl.ds(pl.multiple_of(h * width, 128), width)] = block[...]

    @pl.when(jnp.logical_not(source))
    def _():
        for k in range(pieces):
            landed = out.at[:, columns(h, k)]
            remote(landed, k, side_send, far_recv, partner).wait_recv()
            send_all(landed, k)

    for k in range(pieces):
        mine = block.at[:, pl.ds(k * step, step)]

        @pl.when(up)
        def _():
            remote(mine, k, far_send, far_recv, above).wait_send()

        @pl.when(down)
        def _():
            remote(mine, k, near_send, far_recv, below).wait_send()

        remote(mine, k, side_send, side_recv, partner).wait_send()
        pltpu.make_async_remote_copy(
            src_ref=mine,
            dst_ref=out.at[:, columns(1 - h, k)],
            send_sem=side_send.at[k],
            recv_sem=side_recv.at[k],
            device_id=partner,
            device_id_type=MESH,
        ).wait_recv()


def spread(block, n_q, collective_id):
    maps, width = block.shape
    pieces = width // 128
    vmem = pl.BlockSpec(memory_space=pltpu.VMEM)
    sems = pltpu.SemaphoreType.DMA((pieces,))
    return pl.pallas_call(
        functools.partial(spread_kernel, n_q),
        out_shape=jax.ShapeDtypeStruct((maps, 2 * width), block.dtype),
        in_specs=[vmem],
        out_specs=vmem,
        scratch_shapes=[sems] * 5,
        compiler_params=pltpu.CompilerParams(
            collective_id=collective_id, has_side_effects=True
        ),
        name="spread%d" % collective_id,
    )(block)


def sum_kernel(n, place_of, device_of, x, out, landed, result, send1, recv1, send2, recv2):
    me = place_of()
    barrier = pltpu.get_barrier_semaphore()

    def each(body):
        lax.fori_loop(1, n, lambda k, carry: (body(k), carry)[1], 0)

    def member(k):
        return device_of(lax.rem(me + k, n))

    each(lambda k: pl.semaphore_signal(barrier, inc=1, device_id=member(k), device_id_type=MESH))
    pl.semaphore_wait(barrier, n - 1)

    def scatter(k):
        return pltpu.make_async_remote_copy(
            src_ref=x.at[lax.rem(me + k, n)],
            dst_ref=landed.at[k - 1],
            send_sem=send1.at[k - 1],
            recv_sem=recv1.at[k - 1],
            device_id=member(k),
            device_id_type=MESH,
        )

    def gather(k, slot):
        return pltpu.make_async_remote_copy(
            src_ref=result,
            dst_ref=out.at[slot],
            send_sem=send2.at[k - 1],
            recv_sem=recv2.at[k - 1],
            device_id=member(k),
            device_id_type=MESH,
        )

    each(lambda k: scatter(k).start())
    each(lambda k: scatter(k).wait_recv())
    total = lax.fori_loop(0, n - 1, lambda k, t: t + landed[k], x[me]) if n > 8 else sum(
        (landed[k] for k in range(n - 1)), x[me]
    )
    result[...] = total.astype(result.dtype)
    each(lambda k: gather(k, me).start())
    out[me] = result[...]
    each(lambda k: gather(k, lax.rem(me - k + n, n)).wait_recv())
    each(lambda k: scatter(k).wait_send())
    each(lambda k: gather(k, me).wait_send())


def pair_kernel(
    n, place_of, device_of, x, out, from_pair, pair_sum, landed, result,
    send1, recv1, send2, recv2, send3, recv3, send4, recv4,
):
    me = place_of()
    m = n // 2
    side, spot = me % 2, me // 2
    partner = device_of(me + 1 - 2 * side)

    def member(k):
        return device_of(lax.rem(spot + k, m) * 2 + side)

    def copy(src, dst, send, recv, device):
        return pltpu.make_async_remote_copy(
            src_ref=src, dst_ref=dst, send_sem=send, recv_sem=recv,
            device_id=device, device_id_type=MESH,
        )

    def first(k):
        j = lax.rem(spot + k, m)
        return copy(x.at[2 * j + 1 - side], from_pair.at[j], send1.at[k - 1], recv1.at[k - 1], partner)

    def second(k):
        return copy(pair_sum.at[k - 1], landed.at[k - 1], send2.at[k - 1], recv2.at[k - 1], member(k))

    def third(k, slot):
        return copy(result, out.at[slot], send3.at[k - 1], recv3.at[k - 1], member(k))

    def fourth(k, parity):
        slot = lax.rem(spot - k + m, m) * 2 + parity
        src = result if k == 0 else out.at[slot]
        return copy(src, out.at[slot], send4.at[k], recv4.at[k], partner)

    barrier = pltpu.get_barrier_semaphore()
    pl.semaphore_signal(barrier, inc=1, device_id=partner, device_id_type=MESH)
    for k in range(1, m):
        pl.semaphore_signal(barrier, inc=1, device_id=member(k), device_id_type=MESH)
    pl.semaphore_wait(barrier, m)
    for k in range(1, m + 1):
        first(k).start()
    for k in range(1, m):
        j = lax.rem(spot + k, m)
        first(k).wait_recv()
        pair_sum[k - 1] = x[2 * j + side] + from_pair[j]
        second(k).start()
    first(m).wait_recv()
    total = x[me] + from_pair[spot]
    for k in range(1, m):
        second(k).wait_recv()
        total = total + landed[k - 1]
    result[...] = total.astype(result.dtype)
    for k in range(1, m):
        third(k, me).start()
    fourth(0, side).start()
    out[me] = result[...]
    for k in range(1, m):
        third(k, lax.rem(spot - k + m, m) * 2 + side).wait_recv()
        fourth(k, side).start()
    for k in range(m):
        fourth(k, 1 - side).wait_recv()
    for k in range(1, m + 1):
        first(k).wait_send()
    for k in range(1, m):
        second(k).wait_send()
        third(k, me).wait_send()
    for k in range(m):
        fourth(k, side).wait_send()


def pair_sum_and_share(x, dtype, place_of, device_of, collective_id):
    n, rows, cols = x.shape
    m = n // 2
    vmem = pl.BlockSpec(memory_space=pltpu.VMEM)
    whole, rest = pltpu.SemaphoreType.DMA((m,)), pltpu.SemaphoreType.DMA((m - 1,))
    return pl.pallas_call(
        functools.partial(pair_kernel, n, place_of, device_of),
        out_shape=jax.ShapeDtypeStruct(x.shape, dtype),
        in_specs=[vmem],
        out_specs=vmem,
        scratch_shapes=[
            pltpu.VMEM((m, rows, cols), x.dtype),
            pltpu.VMEM((m - 1, rows, cols), x.dtype),
            pltpu.VMEM((m - 1, rows, cols), x.dtype),
            pltpu.VMEM((rows, cols), dtype),
            whole, whole, rest, rest, rest, rest, whole, whole,
        ],
        compiler_params=pltpu.CompilerParams(
            collective_id=collective_id, has_side_effects=True
        ),
        name="sum%d" % collective_id,
    )(x)


def sum_and_share(x, dtype, place_of, device_of, collective_id):
    n, rows, cols = x.shape
    vmem = pl.BlockSpec(memory_space=pltpu.VMEM)
    sems = pltpu.SemaphoreType.DMA((n - 1,))
    return pl.pallas_call(
        functools.partial(sum_kernel, n, place_of, device_of),
        out_shape=jax.ShapeDtypeStruct(x.shape, dtype),
        in_specs=[vmem],
        out_specs=vmem,
        scratch_shapes=[
            pltpu.VMEM((n - 1, rows, cols), x.dtype),
            pltpu.VMEM((rows, cols), dtype),
            sems, sems, sems, sems,
        ],
        compiler_params=pltpu.CompilerParams(
            collective_id=collective_id, has_side_effects=True
        ),
        name="sum%d" % collective_id,
    )(x)


def per_device(npix, n_rows, n_cols, inverse_cov, cosines, sky_maps):
    maps = sky_maps.shape[1]
    cols_here = inverse_cov.shape[1]
    n_q = n_cols // 2
    sky_rows = spread(sky_maps.T, n_q, 1)
    partial_value = jnp.dot(sky_rows, inverse_cov, preferred_element_type=jnp.float32)
    column_maps = pair_sum_and_share(
        partial_value.reshape(n_rows, maps // n_rows, cols_here),
        jnp.bfloat16,
        lambda: lax.axis_index("prow"),
        lambda i: (i, lax.axis_index("pcol")),
        2,
    ).reshape(maps, cols_here)
    row_maps = spread(column_maps, n_q, 3)
    moments = spectra_moments(cosines, row_maps, column_maps)
    devices = n_rows * n_cols
    matrix, each = transform_matrix(npix, devices)
    partial_spectra = jnp.dot(jnp.asarray(matrix), moments, precision=lax.Precision.HIGHEST)
    shared = sum_and_share(
        partial_spectra.reshape(devices, each, maps),
        jnp.float32,
        lambda: lax.axis_index("prow") * n_cols + lax.axis_index("pcol"),
        lambda i: (i // n_cols, lax.rem(i, n_cols)),
        4,
    )
    spectra = shared.reshape(devices * each, maps)[:L]
    return (row_maps.T, spectra)


def solution(mesh):
    in_specs = (P("prow", "pcol"), P("prow", "pcol"), P("pcol", None))
    out_specs = (P("prow", None), P())
    n_rows, n_cols = mesh.shape["prow"], mesh.shape["pcol"]

    def whole(inverse_cov, cosines, sky_maps):
        npix = cosines.shape[0]
        step = jax.shard_map(
            functools.partial(per_device, npix, n_rows, n_cols),
            mesh=mesh, in_specs=in_specs, out_specs=out_specs, check_vma=False,
        )
        return step(inverse_cov, cosines, sky_maps)

    return whole
```

profile of v0, /device:TPU:0, one launch (start us, length us, event | category | flops | bytes accessed | tf_op | source)
XLA Modules:
  0.0 133.2 jit_solution(6837945594360187986)
XLA Ops:
  0.6 14.8 %spread1.1 = bf16[192,2048]{1,0:T(8,128)(2,1)} custom-call(bf16[192,1024]{1,0:T(8,128)(2,1)} %bitcast.12), custom_call_target="tpu_custom_call" | custom-call | tf_op jit(solution)/shard_map/spread1/pallas_call | solution.py:297
  15.5 0.0 copy-start.3
  15.5 0.0 copy-start.4
  15.5 4.3 %fusion = f32[192,1024]{1,0:T(8,128)} fusion(bf16[192,2048]{1,0:T(8,128)(2,1)} %spread1.1, bf16[2048,1024]{1,0:T(8,128)(2,1)} %param.6), kind=kOutput, calls=%fused_computation | convolution fusion | flops 805306368 | bytes 5767168 | tf_op jit(solution)/shard_map/dot_general | solution.py:475
  19.8 24.7 %sum2.1 = bf16[4,48,1024]{2,1,0:T(8,128)(2,1)} custom-call(f32[4,48,1024]{2,1,0:T(8,128)} %bitcast.11), custom_call_target="tpu_custom_call" | custom-call | tf_op jit(solution)/shard_map/sum2/pallas_call | solution.py:430
  44.5 13.2 %spread3.1.ft = bf16[192,2048]{1,0:T(8,128)(2,1)} custom-call(bf16[192,1024]{1,0:T(8,128)(2,1)} %bitcast.9), custom_call_target="tpu_custom_call" | custom-call | tf_op jit(solution)/shard_map/spread3/pallas_call | solution.py:297
  57.7 0.0 copy-done.3
  57.8 0.0 copy-done.4
  57.8 0.0 copy-start
  57.8 1.1 copy-done
  58.9 0.0 copy-start.2
  58.9 1.0 copy-done.2
  59.9 0.0 copy-start.5
  59.9 0.0 copy-start.1
  59.9 53.8 %moments.1 = f32[66,192]{1,0:T(8,128)S(1)} custom-call(s32[300]{0:T(512)S(1)} %copy-done.3, s32[6]{0:T(128)S(1)} %copy-done.4, f32[2048,1024]{1,0:T(8,128)} %cos_hbm.1, bf16[192,2048]{1,0:T(8,128)(2,1)S(1)} %copy-done, bf16[192,1024]{1,0:T(8,128)(2,1)S(1)} %bitcast.10), custom_call_target="tpu_custom_call" | custom-call | tf_op jit(solution)/shard_map/moments/pallas_call | solution.py:181
  113.7 0.0 copy-done.5
  113.7 0.2 fusion.1
  113.9 0.7 reshape.18.x
  114.6 16.2 %sum4.1 = f32[32,2,192]{2,1,0:T(2,128)} custom-call(f32[32,2,192]{2,1,0:T(2,128)} %reshape.18.x), custom_call_target="tpu_custom_call" | custom-call | tf_op jit(solution)/shard_map/sum4/pallas_call | solution.py:453
  130.8 1.5 %reshape.19 = f32[64,192]{1,0:T(8,128)} reshape(f32[32,2,192]{2,1,0:T(2,128)} %sum4.1) | data formatting | bytes 98304 | tf_op jit(solution)/shard_map/reshape | solution.py:495
  132.3 0.0 copy-done.1
  132.3 0.9 copy.9
Async XLA Ops:
  15.5 42.3 %copy-start.3 = (s32[300]{0:T(512)S(1)}, s32[300]{0:T(512)}, u32[]{:S(2)}) copy-start(s32[300]{0:T(512)} %constant.6.clone.table) | copy-start | bytes 3604
  15.5 42.3 %copy-start.4 = (s32[6]{0:T(128)S(1)}, s32[6]{0:T(128)}, u32[]{:S(2)}) copy-start(s32[6]{0:T(128)} %constant.7.clone.counts) | copy-start | bytes 76
  57.8 1.1 copy-start
  58.9 1.0 copy-start.2
  59.9 53.8 %copy-start.5 = (f32[64,66]{1,0:T(8,128)S(1)}, f32[64,66]{1,0:T(8,128)}, u32[]{:S(2)}) copy-start(f32[64,66]{1,0:T(8,128)} %constant.8.clone) | copy-start | bytes 50692
  59.9 72.4 %copy-start.1 = (bf16[192,2048]{1,0:T(8,128)(2,1)S(1)}, bf16[192,2048]{1,0:T(8,128)(2,1)}, u32[]{:S(2)}) copy-start(bf16[192,2048]{1,0:T(8,128)(2,1)} %spread3.1.ft) | copy-start | bytes 2359300
where the time goes:
time: 134 us; the launch traced here: 133 us
  Pallas kernels  123 us (92%)
  local copies, waits for them, and re-layouts  5.21 us (4%)
  matrix products  4.5 us (3%)
    pallas_call x1, Pallas kernels, spectra_moments(): pl.pallas_call(functools.partial(moments_kernel, stride), out_shape=jax.S...  53.8 us
    pallas_call x2, Pallas kernels, spread(): pl.pallas_call(functools.partial(spread_kernel, n_q), out_shape=jax.Shape...  28.1 us
    pallas_call x1, Pallas kernels, pair_sum_and_share(): pl.pallas_call(functools.partial(pair_kernel, n, place_of, device_of), ou...  24.7 us
    pallas_call x1, Pallas kernels, sum_and_share(): pl.pallas_call(functools.partial(sum_kernel, n, place_of, device_of), out...  16.2 us
    dot_general x1, matrix products, per_device(): jnp.dot(sky_rows, inverse_cov, preferred_element_type=jnp.float32)  4.3 us
    unnamed x13, local copies, waits for them, and re-layouts  3.02 us

commit v1 on v0

--- a/solution.py
+++ b/solution.py
@@ -14,15 +14,22 @@
 LMIN = 2
 TILE = 256
 STRIP = 16
-GROUP = 11
-CHUNKS = 6
-LEVELS = GROUP * CHUNKS
+LOW = 11
+HIGH = 6
+LEVELS = LOW * HIGH
 
 
 def transform_matrix(npix, devices):
     top = LMIN + L - 1
     each = -(-L // devices)
     a = [math.comb(2 * k, k) / 4.0**k for k in range(top + 1)]
+    product = np.zeros((LEVELS, LEVELS))
+    for k in range(LEVELS):
+        high, low = divmod(k, LOW)
+        product[k, low * HIGH + high] = 1
+        if high and low:
+            product[k, low * HIGH + high] = 2
+            product[k] -= product[high * LOW - low]
     out = np.zeros((devices * each, LEVELS))
     for l in range(LMIN, top + 1):
         owner, place = divmod(l - LMIN, each)
@@ -30,7 +37,7 @@
         for k in range(l + 1):
             row[abs(l - 2 * k)] += a[k] * a[l - k]
         row *= (2 * l + 1) / npix
-    return out.astype(np.float32), each
+    return (out @ product).astype(np.float32), each
 
 
 def pair_up(tiles, n):
@@ -79,14 +86,15 @@
 
 
 def moments_kernel(
-    stride, table, counts, cos_hbm, ft, fct, out,
-    xbuf, x2, prev, cur, buf_a, buf_b, lhs, fj, acc, sem,
+    stride, longest, table, counts, cos_hbm, ft, fct, out,
+    xbuf, buf_a, buf_b, lhs, fj, acc, sem,
 ):
     r = lax.axis_index("prow")
     c = lax.axis_index("pcol")
     q, h = c // 2, c % 2
     kind = jnp.where(r > q, h, jnp.where(r < q, 2 + h, 4 + h))
     n_items = counts[kind]
+    n_strips = 2 * TILE // STRIP
 
     def field(item, f):
         return table[(kind * stride + item) * 5 + f]
@@ -96,21 +104,20 @@
         col = pl.multiple_of(field(item, 4) * TILE, TILE)
         return pltpu.make_async_copy(
             cos_hbm.at[pl.ds(row, TILE), pl.ds(col, TILE)],
-            xbuf.at[pl.ds(half * TILE, TILE)],
-            sem.at[half],
+            xbuf.at[item, pl.ds(half * TILE, TILE)],
+            sem.at[item, half],
         )
 
-    def fetch(item):
+    def fetch(item, carry):
         tile_copy(item, 0).start()
         tile_copy(item, 1).start()
-
-    def begin(item):
-        tile_copy(item, 0).wait()
-        tile_copy(item, 1).wait()
-        x = xbuf[...]
-        x2[...] = x + x
-        prev[...] = (x + x) * x - 1.0
-        cur[...] = x
+        return carry
+
+    def landed(item):
+        @pl.when(item < n_items)
+        def _():
+            tile_copy(item, 0).wait()
+            tile_copy(item, 1).wait()
 
     def set_operands(item):
         col = pl.multiple_of(field(item, 4) * TILE, TILE)
@@ -121,54 +128,67 @@
             lhs[:, half * TILE : (half + 1) * TILE] = value.astype(jnp.bfloat16)
         fj[...] = fct[:, pl.ds(col, TILE)].astype(jnp.float32)
 
-    n_strips = 2 * TILE // STRIP
-
-    def gen_strip(buf, s):
-        rows = pl.ds(s * STRIP, STRIP)
-        xx = x2[rows, :]
-        p = prev[rows, :]
-        t = cur[rows, :]
-        for g in range(GROUP):
+    def gen_strip(buf, item, s):
+        rows = pl.ds(pl.multiple_of(s * STRIP, STRIP), STRIP)
+        x = xbuf[item, rows, :]
+        xx = x + x
+        buf[1, rows, :] = x.astype(jnp.bfloat16)
+        p, t = x, xx * x - 1.0
+        for k in range(2, LOW):
+            buf[k, rows, :] = t.astype(jnp.bfloat16)
             p, t = t, xx * t - p
-            buf[g, rows, :] = t.astype(jnp.bfloat16)
-        prev[rows, :] = p
-        cur[rows, :] = t
-
-    def half_step(gen, use, level0):
+        yy = t + t
+        buf[LOW, rows, :] = t.astype(jnp.bfloat16)
+        p, t = t, yy * t - 1.0
+        for k in range(2, HIGH):
+            buf[LOW + k - 1, rows, :] = t.astype(jnp.bfloat16)
+            p, t = t, yy * t - p
+
+    def item_pass(item, use, gen):
+        following = jnp.minimum(item + 1, n_items - 1)
+        landed(item + 1)
+        set_operands(item)
+
+        half_tile = TILE // 2
         done = 0
-        for g in range(GROUP):
-            upto = (g + 1) * n_strips // GROUP
+        for level in range(LEVELS):
+            k, g = divmod(level, HIGH)
+            upto = (level + 1) * n_strips // LEVELS
             for s in range(done, upto):
-                gen_strip(gen, s)
+                gen_strip(gen, following, s)
             done = upto
-            image = jnp.dot(lhs[...], use[g], preferred_element_type=jnp.float32)
+            if k == 0:
+                rhs = use[LOW + g - 1] if g else use[0]
+            else:
+                rhs = use[LOW + g - 1] * use[k] if g else use[k]
+            image = jnp.dot(lhs[...], rhs, preferred_element_type=jnp.float32)
             prod = image * fj[...]
-            half_tile = TILE // 2
-            acc[level0 + g] += prod[:, :half_tile] + prod[:, half_tile:]
-
+            folded = prod[:, :half_tile] + prod[:, half_tile:]
+            acc[level] += folded
+            xbuf[longest, 0:8, 0:half_tile] = folded[0:8, :]
+
+    lax.fori_loop(0, n_items, fetch, 0)
     acc[...] = jnp.zeros_like(acc)
-    fetch(0)
-    begin(0)
-    for s in range(n_strips):
-        gen_strip(buf_a, s)
-
-    def item_loop(item, carry):
-        fetch(item + 1)
-        set_operands(item)
-
-        def chunk_loop(cp, carry):
-            half_step(buf_b, buf_a, cp * 2 * GROUP)
-
-            @pl.when(cp == CHUNKS // 2 - 1)
-            def _():
-                begin(item + 1)
-
-            half_step(buf_a, buf_b, cp * 2 * GROUP + GROUP)
-            return carry
-
-        return lax.fori_loop(0, CHUNKS // 2, chunk_loop, carry)
-
-    lax.fori_loop(0, n_items, item_loop, 0)
+    for buf in (buf_a, buf_b):
+        buf[0] = jnp.ones(buf.shape[1:], buf.dtype)
+    landed(0)
+
+    def first(s, carry):
+        gen_strip(buf_a, 0, s)
+        return carry
+
+    lax.fori_loop(0, n_strips, first, 0, unroll=4)
+
+    def two_items(pair, carry):
+        item_pass(2 * pair, buf_a, buf_b)
+
+        @pl.when(2 * pair + 1 < n_items)
+        def _():
+            item_pass(2 * pair + 1, buf_b, buf_a)
+
+        return carry
+
+    lax.fori_loop(0, (n_items + 1) // 2, two_items, 0)
     out[...] = jnp.sum(acc[...], axis=-1)
 
 
@@ -176,24 +196,22 @@
     maps = ft.shape[0]
     n = cosines.shape[1] // TILE
     table, counts, stride = work_tables(n)
+    longest = int(counts.max())
     vmem = pl.BlockSpec(memory_space=pltpu.VMEM)
     smem = pl.BlockSpec(memory_space=pltpu.SMEM)
     return pl.pallas_call(
-        functools.partial(moments_kernel, stride),
+        functools.partial(moments_kernel, stride, longest),
         out_shape=jax.ShapeDtypeStruct((LEVELS, maps), jnp.float32),
         in_specs=[smem, smem, pl.BlockSpec(memory_space=pl.ANY), vmem, vmem],
         out_specs=vmem,
         scratch_shapes=[
-            pltpu.VMEM((2 * TILE, TILE), jnp.float32),
-            pltpu.VMEM((2 * TILE, TILE), jnp.float32),
-            pltpu.VMEM((2 * TILE, TILE), jnp.float32),
-            pltpu.VMEM((2 * TILE, TILE), jnp.float32),
-            pltpu.VMEM((GROUP, 2 * TILE, TILE), jnp.bfloat16),
-            pltpu.VMEM((GROUP, 2 * TILE, TILE), jnp.bfloat16),
+            pltpu.VMEM((longest + 1, 2 * TILE, TILE), jnp.float32),
+            pltpu.VMEM((LOW + HIGH - 1, 2 * TILE, TILE), jnp.bfloat16),
+            pltpu.VMEM((LOW + HIGH - 1, 2 * TILE, TILE), jnp.bfloat16),
             pltpu.VMEM((maps, 2 * TILE), jnp.bfloat16),
             pltpu.VMEM((maps, TILE), jnp.float32),
             pltpu.VMEM((LEVELS, maps, TILE // 2), jnp.float32),
-            pltpu.SemaphoreType.DMA((2,)),
+            pltpu.SemaphoreType.DMA((longest, 2)),
         ],
         compiler_params=pltpu.CompilerParams(vmem_limit_bytes=48 * 2**20),
         name="moments",

time: 134 us -> 121 us (0.903)
  Pallas kernels: 123 us -> 110 us
    pallas_call x1, Pallas kernels: 53.8 us -> 39.2 us  [spectra_moments(): pl.pallas_call(functools.partial(moments_kernel, stride, longest), out_sh...]
    pallas_call x1, Pallas kernels: 16.2 us -> 17.9 us  [sum_and_share(): pl.pallas_call(functools.partial(sum_kernel, n, place_of, device_of), out...]
where the time goes in v1:
time: 121 us; the launch traced here: 120 us
  Pallas kernels  110 us (91%)
  local copies, waits for them, and re-layouts  5.21 us (4%)
  matrix products  4.5 us (4%)
    pallas_call x1, Pallas kernels, spectra_moments(): pl.pallas_call(functools.partial(moments_kernel, stride, longest), out_sh...  39.2 us
    pallas_call x2, Pallas kernels, spread(): pl.pallas_call(functools.partial(spread_kernel, n_q), out_shape=jax.Shape...  28.1 us
    pallas_call x1, Pallas kernels, pair_sum_and_share(): pl.pallas_call(functools.partial(pair_kernel, n, place_of, device_of), ou...  24.7 us
    pallas_call x1, Pallas kernels, sum_and_share(): pl.pallas_call(functools.partial(sum_kernel, n, place_of, device_of), out...  17.9 us
    dot_general x1, matrix products, per_device(): jnp.dot(sky_rows, inverse_cov, preferred_element_type=jnp.float32)  4.3 us
    unnamed x13, local copies, waits for them, and re-layouts  3.02 us

profile of v1, /device:TPU:0, one launch (start us, length us, event | category | flops | bytes accessed | tf_op | source)
XLA Modules:
  0.0 120.2 jit_solution(17332136107314062650)
XLA Ops:
  0.6 14.8 %spread1.1 = bf16[192,2048]{1,0:T(8,128)(2,1)} custom-call(bf16[192,1024]{1,0:T(8,128)(2,1)} %bitcast.12), custom_call_target="tpu_custom_call" | custom-call | tf_op jit(solution)/shard_map/spread1/pallas_call | solution.py:315
  15.5 0.0 copy-start.3
  15.5 0.0 copy-start.4
  15.5 4.3 %fusion = f32[192,1024]{1,0:T(8,128)} fusion(bf16[192,2048]{1,0:T(8,128)(2,1)} %spread1.1, bf16[2048,1024]{1,0:T(8,128)(2,1)} %param.6), kind=kOutput, calls=%fused_computation | convolution fusion | flops 805306368 | bytes 5767168 | tf_op jit(solution)/shard_map/dot_general | solution.py:493
  19.8 24.7 %sum2.1 = bf16[4,48,1024]{2,1,0:T(8,128)(2,1)} custom-call(f32[4,48,1024]{2,1,0:T(8,128)} %bitcast.11), custom_call_target="tpu_custom_call" | custom-call | tf_op jit(solution)/shard_map/sum2/pallas_call | solution.py:448
  44.5 13.2 %spread3.1.ft = bf16[192,2048]{1,0:T(8,128)(2,1)} custom-call(bf16[192,1024]{1,0:T(8,128)(2,1)} %bitcast.9), custom_call_target="tpu_custom_call" | custom-call | tf_op jit(solution)/shard_map/spread3/pallas_call | solution.py:315
  57.7 0.0 copy-done.3
  57.8 0.0 copy-done.4
  57.8 0.0 copy-start
  57.8 1.1 copy-done
  58.9 0.0 copy-start.2
  58.9 1.0 copy-done.2
  59.9 0.0 copy-start.5
  59.9 0.0 copy-start.1
  59.9 39.2 %moments.1 = f32[66,192]{1,0:T(8,128)S(1)} custom-call(s32[300]{0:T(512)S(1)} %copy-done.3, s32[6]{0:T(128)S(1)} %copy-done.4, f32[2048,1024]{1,0:T(8,128)} %cos_hbm.1, bf16[192,2048]{1,0:T(8,128)(2,1)S(1)} %copy-done, bf16[192,1024]{1,0:T(8,128)(2,1)S(1)} %bitcast.10), custom_call_target="tpu_custom_call" | custom-call | tf_op jit(solution)/shard_map/moments/pallas_call | solution.py:202
  99.1 0.0 copy-done.5
  99.1 0.2 fusion.1
  99.3 0.7 reshape.18.x
  100.0 17.9 %sum4.1 = f32[32,2,192]{2,1,0:T(2,128)} custom-call(f32[32,2,192]{2,1,0:T(2,128)} %reshape.18.x), custom_call_target="tpu_custom_call" | custom-call | tf_op jit(solution)/shard_map/sum4/pallas_call | solution.py:471
  117.8 1.5 %reshape.19 = f32[64,192]{1,0:T(8,128)} reshape(f32[32,2,192]{2,1,0:T(2,128)} %sum4.1) | data formatting | bytes 98304 | tf_op jit(solution)/shard_map/reshape | solution.py:513
  119.3 0.0 copy-done.1
  119.3 0.9 copy.9
Async XLA Ops:
  15.5 42.3 %copy-start.3 = (s32[300]{0:T(512)S(1)}, s32[300]{0:T(512)}, u32[]{:S(2)}) copy-start(s32[300]{0:T(512)} %constant.6.clone.table) | copy-start | bytes 3604
  15.5 42.3 %copy-start.4 = (s32[6]{0:T(128)S(1)}, s32[6]{0:T(128)}, u32[]{:S(2)}) copy-start(s32[6]{0:T(128)} %constant.7.clone.counts) | copy-start | bytes 76
  57.8 1.1 copy-start
  58.9 1.0 copy-start.2
  59.9 39.2 %copy-start.5 = (f32[64,66]{1,0:T(8,128)S(1)}, f32[64,66]{1,0:T(8,128)}, u32[]{:S(2)}) copy-start(f32[64,66]{1,0:T(8,128)} %constant.8.clone) | copy-start | bytes 50692
  59.9 59.4 %copy-start.1 = (bf16[192,2048]{1,0:T(8,128)(2,1)S(1)}, bf16[192,2048]{1,0:T(8,128)(2,1)}, u32[]{:S(2)}) copy-start(bf16[192,2048]{1,0:T(8,128)(2,1)} %spread3.1.ft) | copy-start | bytes 2359300

commit v2 on v1

--- a/solution.py
+++ b/solution.py
@@ -219,110 +219,215 @@
 
 
 MESH = pl.DeviceIdType.MESH
-
-
-def spread_kernel(n_q, block, out, far_send, near_send, far_recv, side_send, side_recv):
+CHUNKS = 4
+
+
+def weigh_kernel(
+    n_rows, n_q, sky, cov_hbm, ft, fct,
+    cov, x_out, x_in, mine, z_out, z_in,
+    cov_sem, x_send, x_recv, z_send, z_recv, a_send, a_recv, p_send, p_recv, c_send, c_recv,
+):
     r = lax.axis_index("prow")
     c = lax.axis_index("pcol")
     q, h = c // 2, c % 2
-    width = block.shape[1]
-    pieces = far_recv.shape[0]
-    step = width // pieces
+    maps = sky.shape[0]
+    group = maps // n_q
+    half = cov.shape[0] // 2
+    width = half // CHUNKS
     partner = (r, c + 1 - 2 * h)
-    above, below = (r, c + 2), (r, c - 2)
-    has_above, has_below = q < n_q - 1, q > 0
+    diagonal = r == q
+
+    def line(k):
+        return lax.rem(q + k, n_q)
+
+    def other(k):
+        return lax.rem(r + k, n_rows)
+
+    def at(j):
+        return pl.ds(j * width, width)
+
+    def placed(j):
+        return pl.ds(pl.multiple_of(h * half + j * width, width), width)
+
+    def cov_copy(j, own):
+        side = h if own else 1 - h
+        return pltpu.make_async_copy(
+            cov_hbm.at[pl.ds(pl.multiple_of(side * half + j * width, width), width)],
+            cov.at[pl.ds((int(own) * CHUNKS + j) * width, width)],
+            cov_sem.at[int(own) * CHUNKS + j],
+        )
+
+    def copy(src, dst, send, recv, device):
+        return pltpu.make_async_remote_copy(
+            src_ref=src, dst_ref=dst, send_sem=send, recv_sem=recv,
+            device_id=device, device_id_type=MESH,
+        )
+
+    def x_copy(j):
+        return copy(x_out.at[j], x_in.at[j], x_send.at[j], x_recv.at[j], partner)
+
+    def z_copy(j, k):
+        return copy(
+            z_out.at[line(k), :, at(j)], z_in.at[k - 1, :, at(j)],
+            z_send.at[j, k - 1], z_recv.at[j, k - 1], (r, line(k) * 2 + h),
+        )
+
+    def a_copy(j, k):
+        return copy(
+            ft.at[q, :, placed(j)], ft.at[q, :, placed(j)],
+            a_send.at[j, k - 1], a_recv.at[j, k - 1], (r, line(k) * 2 + h),
+        )
+
+    def a_arrival(j, k):
+        g = line(n_q - k)
+        return g, copy(
+            ft.at[g, :, placed(j)], ft.at[g, :, placed(j)],
+            a_send.at[j, k - 1], a_recv.at[j, k - 1], partner,
+        )
+
+    def p_copy(j, g, slot):
+        return copy(
+            ft.at[g, :, placed(j)], ft.at[g, :, placed(j)],
+            p_send.at[j, slot], p_recv.at[j, slot], partner,
+        )
+
+    def c_copy(j, g, slot, k):
+        return copy(
+            ft.at[g, :, placed(j)], fct.at[g, :, at(j)],
+            c_send.at[j, slot, k - 1], c_recv.at[j, slot], (other(k), c),
+        )
+
+    def product(j, own):
+        cov_copy(j, own).wait()
+        block = cov[(int(own) * CHUNKS + j) * width : (int(own) * CHUNKS + j + 1) * width, :]
+        return lax.dot_general(
+            sky[...], block, (((1,), (1,)), ((), ())), preferred_element_type=jnp.float32
+        )
+
+    def share(j, g, slot):
+        @pl.when(diagonal)
+        def _():
+            for k in range(1, n_rows):
+                c_copy(j, g, slot, k).start()
+
+        p_copy(j, g, slot).start()
+
+    for own in (False, True):
+        for j in range(CHUNKS):
+            cov_copy(j, own).start()
     barrier = pltpu.get_barrier_semaphore()
-    pl.semaphore_signal(barrier, inc=1, device_id=partner, device_id_type=MESH)
-
-    @pl.when(has_above)
+    greeted = [partner]
+    greeted += [(r, line(k) * 2 + h) for k in range(1, n_q)]
+    greeted += [(other(k), c) for k in range(1, n_rows)]
+    for device in greeted:
+        pl.semaphore_signal(barrier, inc=1, device_id=device, device_id_type=MESH)
+    for j in range(CHUNKS):
+        x_out[j] = product(j, False).astype(x_out.dtype)
+        if j == 0:
+            pl.semaphore_wait(barrier, len(greeted))
+        x_copy(j).start()
+    for j in range(CHUNKS):
+        total = product(j, True)
+        for g in range(n_q):
+            mine[g, :, j * width : (j + 1) * width] = total[g * group : (g + 1) * group]
+    for j in range(CHUNKS):
+        x_copy(j).wait_recv()
+        for g in range(n_q):
+            total = mine[g, :, j * width : (j + 1) * width] + x_in[j, g * group : (g + 1) * group]
+            mine[g, :, j * width : (j + 1) * width] = total
+            z_out[g, :, j * width : (j + 1) * width] = total.astype(z_out.dtype)
+        for k in range(1, n_q):
+            z_copy(j, k).start()
+    lag = min(2, CHUNKS)
+    for step in range(CHUNKS + lag):
+        if step < CHUNKS:
+            j = step
+            total = mine[q, :, j * width : (j + 1) * width]
+            for k in range(1, n_q):
+                z_copy(j, k).wait_recv()
+                total = total + z_in[k - 1, :, j * width : (j + 1) * width]
+            ft[q, :, placed(j)] = total.astype(ft.dtype)
+            for k in range(1, n_q):
+                a_copy(j, k).start()
+            share(j, q, 0)
+        if step >= lag:
+            j = step - lag
+            for k in range(1, n_q):
+                g, arrival = a_arrival(j, k)
+                arrival.wait_recv()
+                share(j, g, k)
+
+    def mirrored(slot):
+        return q if slot == 0 else line(n_q - slot)
+
+    @pl.when(diagonal)
     def _():
-        pl.semaphore_signal(barrier, inc=1, device_id=above, device_id_type=MESH)
-
-    @pl.when(has_below)
+        fct[...] = ft[:, :, pl.ds(pl.multiple_of(h * half, half), half)]
+        for j in range(CHUNKS):
+            for slot in range(n_q):
+                for k in range(1, n_rows):
+                    c_copy(j, mirrored(slot), slot, k).wait_send()
+
+    @pl.when(jnp.logical_not(diagonal))
     def _():
-        pl.semaphore_signal(barrier, inc=1, device_id=below, device_id_type=MESH)
-
-    pl.semaphore_wait(barrier, 1 + has_above.astype(jnp.int32) + has_below.astype(jnp.int32))
-
-    source = q == r
-    up = jnp.logical_and(q >= r, has_above)
-    down = jnp.logical_and(q <= r, has_below)
-
-    def columns(half, k):
-        return pl.ds(pl.multiple_of(half * width + k * step, 128), step)
-
-    def remote(src, k, send, recv, device):
-        return pltpu.make_async_remote_copy(
-            src_ref=src,
-            dst_ref=out.at[:, columns(h, k)],
-            send_sem=send.at[k],
-            recv_sem=recv.at[k],
-            device_id=device,
-            device_id_type=MESH,
-        )
-
-    def send_all(src, k):
-        @pl.when(up)
-        def _():
-            remote(src, k, far_send, far_recv, above).start()
-
-        @pl.when(down)
-        def _():
-            remote(src, k, near_send, far_recv, below).start()
-
-        remote(src, k, side_send, side_recv, partner).start()
-
-    @pl.when(source)
-    def _():
-        for k in range(pieces):
-            send_all(block.at[:, pl.ds(k * step, step)], k)
-        out[:, pl.ds(pl.multiple_of(h * width, 128), width)] = block[...]
-
-    @pl.when(jnp.logical_not(source))
-    def _():
-        for k in range(pieces):
-            landed = out.at[:, columns(h, k)]
-            remote(landed, k, side_send, far_recv, partner).wait_recv()
-            send_all(landed, k)
-
-    for k in range(pieces):
-        mine = block.at[:, pl.ds(k * step, step)]
-
-        @pl.when(up)
-        def _():
-            remote(mine, k, far_send, far_recv, above).wait_send()
-
-        @pl.when(down)
-        def _():
-            remote(mine, k, near_send, far_recv, below).wait_send()
-
-        remote(mine, k, side_send, side_recv, partner).wait_send()
-        pltpu.make_async_remote_copy(
-            src_ref=mine,
-            dst_ref=out.at[:, columns(1 - h, k)],
-            send_sem=side_send.at[k],
-            recv_sem=side_recv.at[k],
-            device_id=partner,
-            device_id_type=MESH,
-        ).wait_recv()
-
-
-def spread(block, n_q, collective_id):
-    maps, width = block.shape
-    pieces = width // 128
+        for j in range(CHUNKS):
+            for slot in range(n_q):
+                copy(
+                    ft.at[q, :, placed(j)], fct.at[mirrored(slot), :, at(j)],
+                    c_send.at[j, slot, 0], c_recv.at[j, slot], partner,
+                ).wait_recv()
+
+    for j in range(CHUNKS):
+        x_copy(j).wait_send()
+        for k in range(1, n_q):
+            z_copy(j, k).wait_send()
+            a_copy(j, k).wait_send()
+        for slot in range(n_q):
+            g = mirrored(slot)
+            outward = p_copy(j, g, slot)
+            outward.wait_send()
+            elsewhere = pl.ds(pl.multiple_of((1 - h) * half + j * width, width), width)
+            copy(
+                ft.at[g, :, elsewhere], ft.at[g, :, elsewhere],
+                p_send.at[j, slot], p_recv.at[j, slot], partner,
+            ).wait_recv()
+
+
+def weigh(sky, cov, n_rows, n_q):
+    maps, depth = sky.shape
+    rows = cov.shape[0]
+    half = rows // 2
+    width = half // CHUNKS
+    group = maps // n_q
     vmem = pl.BlockSpec(memory_space=pltpu.VMEM)
-    sems = pltpu.SemaphoreType.DMA((pieces,))
+    dma = pltpu.SemaphoreType.DMA
     return pl.pallas_call(
-        functools.partial(spread_kernel, n_q),
-        out_shape=jax.ShapeDtypeStruct((maps, 2 * width), block.dtype),
-        in_specs=[vmem],
-        out_specs=vmem,
-        scratch_shapes=[sems] * 5,
+        functools.partial(weigh_kernel, n_rows, n_q),
+        out_shape=[
+            jax.ShapeDtypeStruct((n_q, group, rows), jnp.bfloat16),
+            jax.ShapeDtypeStruct((n_q, group, half), jnp.bfloat16),
+        ],
+        in_specs=[vmem, pl.BlockSpec(memory_space=pl.ANY)],
+        out_specs=[vmem, vmem],
+        scratch_shapes=[
+            pltpu.VMEM((rows, depth), jnp.bfloat16),
+            pltpu.VMEM((CHUNKS, maps, width), jnp.bfloat16),
+            pltpu.VMEM((CHUNKS, maps, width), jnp.bfloat16),
+            pltpu.VMEM((n_q, group, half), jnp.float32),
+            pltpu.VMEM((n_q, group, half), jnp.bfloat16),
+            pltpu.VMEM((n_q - 1, group, half), jnp.bfloat16),
+            dma((2 * CHUNKS,)),
+            dma((CHUNKS,)), dma((CHUNKS,)),
+            dma((CHUNKS, n_q - 1)), dma((CHUNKS, n_q - 1)),
+            dma((CHUNKS, n_q - 1)), dma((CHUNKS, n_q - 1)),
+            dma((CHUNKS, n_q)), dma((CHUNKS, n_q)),
+            dma((CHUNKS, n_q, n_rows - 1)), dma((CHUNKS, n_q)),
+        ],
         compiler_params=pltpu.CompilerParams(
-            collective_id=collective_id, has_side_effects=True
+            collective_id=1, has_side_effects=True, vmem_limit_bytes=32 * 2**20
         ),
-        name="spread%d" % collective_id,
-    )(block)
+        name="weigh",
+    )(sky, cov)
 
 
 def sum_kernel(n, place_of, device_of, x, out, landed, result, send1, recv1, send2, recv2):
@@ -369,99 +474,6 @@
     each(lambda k: gather(k, lax.rem(me - k + n, n)).wait_recv())
     each(lambda k: scatter(k).wait_send())
     each(lambda k: gather(k, me).wait_send())
-
-
-def pair_kernel(
-    n, place_of, device_of, x, out, from_pair, pair_sum, landed, result,
-    send1, recv1, send2, recv2, send3, recv3, send4, recv4,
-):
-    me = place_of()
-    m = n // 2
-    side, spot = me % 2, me // 2
-    partner = device_of(me + 1 - 2 * side)
-
-    def member(k):
-        return device_of(lax.rem(spot + k, m) * 2 + side)
-
-    def copy(src, dst, send, recv, device):
-        return pltpu.make_async_remote_copy(
-            src_ref=src, dst_ref=dst, send_sem=send, recv_sem=recv,
-            device_id=device, device_id_type=MESH,
-        )
-
-    def first(k):
-        j = lax.rem(spot + k, m)
-        return copy(x.at[2 * j + 1 - side], from_pair.at[j], send1.at[k - 1], recv1.at[k - 1], partner)
-
-    def second(k):
-        return copy(pair_sum.at[k - 1], landed.at[k - 1], send2.at[k - 1], recv2.at[k - 1], member(k))
-
-    def third(k, slot):
-        return copy(result, out.at[slot], send3.at[k - 1], recv3.at[k - 1], member(k))
-
-    def fourth(k, parity):
-        slot = lax.rem(spot - k + m, m) * 2 + parity
-        src = result if k == 0 else out.at[slot]
-        return copy(src, out.at[slot], send4.at[k], recv4.at[k], partner)
-
-    barrier = pltpu.get_barrier_semaphore()
-    pl.semaphore_signal(barrier, inc=1, device_id=partner, device_id_type=MESH)
-    for k in range(1, m):
-        pl.semaphore_signal(barrier, inc=1, device_id=member(k), device_id_type=MESH)
-    pl.semaphore_wait(barrier, m)
-    for k in range(1, m + 1):
-        first(k).start()
-    for k in range(1, m):
-        j = lax.rem(spot + k, m)
-        first(k).wait_recv()
-        pair_sum[k - 1] = x[2 * j + side] + from_pair[j]
-        second(k).start()
-    first(m).wait_recv()
-    total = x[me] + from_pair[spot]
-    for k in range(1, m):
-        second(k).wait_recv()
-        total = total + landed[k - 1]
-    result[...] = total.astype(result.dtype)
-    for k in range(1, m):
-        third(k, me).start()
-    fourth(0, side).start()
-    out[me] = result[...]
-    for k in range(1, m):
-        third(k, lax.rem(spot - k + m, m) * 2 + side).wait_recv()
-        fourth(k, side).start()
-    for k in range(m):
-        fourth(k, 1 - side).wait_recv()
-    for k in range(1, m + 1):
-        first(k).wait_send()
-    for k in range(1, m):
-        second(k).wait_send()
-        third(k, me).wait_send()
-    for k in range(m):
-        fourth(k, side).wait_send()
-
-
-def pair_sum_and_share(x, dtype, place_of, device_of, collective_id):
-    n, rows, cols = x.shape
-    m = n // 2
-    vmem = pl.BlockSpec(memory_space=pltpu.VMEM)
-    whole, rest = pltpu.SemaphoreType.DMA((m,)), pltpu.SemaphoreType.DMA((m - 1,))
-    return pl.pallas_call(
-        functools.partial(pair_kernel, n, place_of, device_of),
-        out_shape=jax.ShapeDtypeStruct(x.shape, dtype),
-        in_specs=[vmem],
-        out_specs=vmem,
-        scratch_shapes=[
-            pltpu.VMEM((m, rows, cols), x.dtype),
-            pltpu.VMEM((m - 1, rows, cols), x.dtype),
-            pltpu.VMEM((m - 1, rows, cols), x.dtype),
-            pltpu.VMEM((rows, cols), dtype),
-            whole, whole, rest, rest, rest, rest, whole, whole,
-        ],
-        compiler_params=pltpu.CompilerParams(
-            collective_id=collective_id, has_side_effects=True
-        ),
-        name="sum%d" % collective_id,
-    )(x)
 
 
 def sum_and_share(x, dtype, place_of, device_of, collective_id):
@@ -487,18 +499,10 @@
 
 def per_device(npix, n_rows, n_cols, inverse_cov, cosines, sky_maps):
     maps = sky_maps.shape[1]
-    cols_here = inverse_cov.shape[1]
     n_q = n_cols // 2
-    sky_rows = spread(sky_maps.T, n_q, 1)
-    partial_value = jnp.dot(sky_rows, inverse_cov, preferred_element_type=jnp.float32)
-    column_maps = pair_sum_and_share(
-        partial_value.reshape(n_rows, maps // n_rows, cols_here),
-        jnp.bfloat16,
-        lambda: lax.axis_index("prow"),
-        lambda i: (i, lax.axis_index("pcol")),
-        2,
-    ).reshape(maps, cols_here)
-    row_maps = spread(column_maps, n_q, 3)
+    ft, fct = weigh(sky_maps.T, inverse_cov, n_rows, n_q)
+    row_maps = ft.reshape(maps, ft.shape[2])
+    column_maps = fct.reshape(maps, fct.shape[2])
     moments = spectra_moments(cosines, row_maps, column_maps)
     devices = n_rows * n_cols
     matrix, each = transform_matrix(npix, devices)

time: 121 us -> 96.7 us (0.80)
  Pallas kernels: 110 us -> 87.9 us
  matrix products: 4.5 us -> 0.19 us
  local copies, waits for them, and re-layouts: 5.21 us -> 7.57 us
    pallas_call x3 -> x1, Pallas kernels: 52.8 us -> 33.7 us  [weigh(): pl.pallas_call(functools.partial(weigh_kernel, n_rows, n_q), out_shape=[j...]
    dot_general x1 -> x0, matrix products: 4.3 us -> none  [per_device(): jnp.dot(sky_rows, inverse_cov, preferred_element_type=jnp.float32)]
    pallas_call x1, Pallas kernels: 17.9 us -> 15.1 us  [sum_and_share(): pl.pallas_call(functools.partial(sum_kernel, n, place_of, device_of), out...]
    unnamed x13 -> x11, local copies, waits for them, and re-layouts: 3.02 us -> 5.39 us
where the time goes in v2:
time: 96.7 us; the launch traced here: 96.4 us
  Pallas kernels  87.9 us (91%)
  local copies, waits for them, and re-layouts  7.57 us (8%)
    pallas_call x1, Pallas kernels, spectra_moments(): pl.pallas_call(functools.partial(moments_kernel, stride, longest), out_sh...  39.1 us
    pallas_call x1, Pallas kernels, weigh(): pl.pallas_call(functools.partial(weigh_kernel, n_rows, n_q), out_shape=[j...  33.7 us
    pallas_call x1, Pallas kernels, sum_and_share(): pl.pallas_call(functools.partial(sum_kernel, n, place_of, device_of), out...  15.1 us
    unnamed x11, local copies, waits for them, and re-layouts  5.39 us

profile of v2, /device:TPU:0, one launch (start us, length us, event | category | flops | bytes accessed | tf_op | source)
XLA Modules:
  0.0 96.4 jit_solution(13190356446397896880)
XLA Ops:
  0.6 0.0 copy-start
  0.6 2.2 %copy-done = bf16[2048,1024]{1,0:T(8,128)(2,1)S(1)} copy-done((bf16[2048,1024]{1,0:T(8,128)(2,1)S(1)}, bf16[2048,1024]{1,0:T(8,128)(2,1)}, u32[]{:S(2)}) %copy-start) | copy-done | bytes 4194328
  2.8 0.0 copy-start.1
  2.8 1.0 %copy-done.1 = bf16[1024,192]{0,1:T(8,128)(2,1)S(1)} copy-done((bf16[1024,192]{0,1:T(8,128)(2,1)S(1)}, bf16[1024,192]{0,1:T(8,128)(2,1)}, u32[]{:S(2)}) %copy-start.1) | copy-done | bytes 393240
  3.8 0.0 copy-start.4
  3.8 33.7 %weigh.1 = (bf16[4,48,2048]{2,1,0:T(8,128)(2,1)S(1)}, bf16[4,48,1024]{2,1,0:T(8,128)(2,1)S(1)}) custom-call(bf16[192,1024]{1,0:T(8,128)(2,1)S(1)} %bitcast.10, bf16[2048,1024]{1,0:T(8,128)(2,1)S(1)} %copy-done), custom_call_target="tpu_custom_call" | custom-call | tf_op jit(solution)/shard_map/weigh/pallas_call | solution.py:404
  37.5 0.0 copy-start.2
  37.5 0.7 copy-done.2
  38.2 0.0 copy-start.3
  38.2 0.7 copy-done.3
  38.9 39.1 %moments.1 = f32[66,192]{1,0:T(8,128)S(1)} custom-call(s32[300]{0:T(512)S(1)} %copy-done.2, s32[6]{0:T(128)S(1)} %copy-done.3, f32[2048,1024]{1,0:T(8,128)} %cos_hbm.1, bf16[192,2048]{1,0:T(8,128)(2,1)S(1)} %bitcast.7, bf16[192,1024]{1,0:T(8,128)(2,1)S(1)} %bitcast.9), custom_call_target="tpu_custom_call" | custom-call | tf_op jit(solution)/shard_map/moments/pallas_call | solution.py:202
  78.0 0.0 copy-done.4
  78.0 0.2 fusion
  78.2 0.7 reshape.18.x
  78.9 15.1 %sum4.1 = f32[32,2,192]{2,1,0:T(2,128)} custom-call(f32[32,2,192]{2,1,0:T(2,128)} %reshape.18.x), custom_call_target="tpu_custom_call" | custom-call | tf_op jit(solution)/shard_map/sum4/pallas_call | solution.py:483
  94.0 1.5 %reshape.19 = f32[64,192]{1,0:T(8,128)} reshape(f32[32,2,192]{2,1,0:T(2,128)} %sum4.1) | data formatting | bytes 98304 | tf_op jit(solution)/shard_map/reshape | solution.py:517
  95.5 0.9 copy.9
Async XLA Ops:
  0.6 2.2 %copy-start = (bf16[2048,1024]{1,0:T(8,128)(2,1)S(1)}, bf16[2048,1024]{1,0:T(8,128)(2,1)}, u32[]{:S(2)}) copy-start(bf16[2048,1024]{1,0:T(8,128)(2,1)} %cov_hbm.1) | copy-start | bytes 12582916
  2.8 1.0 %copy-start.1 = (bf16[1024,192]{0,1:T(8,128)(2,1)S(1)}, bf16[1024,192]{0,1:T(8,128)(2,1)}, u32[]{:S(2)}) copy-start(bf16[1024,192]{0,1:T(8,128)(2,1)} %param.8) | copy-start | bytes 1179652
  3.8 74.2 %copy-start.4 = (f32[64,66]{1,0:T(8,128)S(1)}, f32[64,66]{1,0:T(8,128)}, u32[]{:S(2)}) copy-start(f32[64,66]{1,0:T(8,128)} %constant.8.clone) | copy-start | bytes 50692
  37.5 0.7 copy-start.2
  38.2 0.7 copy-start.3

commit v3 on v2

v3 whole, which is shorter than its diff:
```python
import functools
import math

import jax
import jax.numpy as jnp
import numpy as np
from jax import lax
from jax.experimental import pallas as pl
from jax.experimental.pallas import tpu as pltpu
from jax.sharding import PartitionSpec as P

L = 64
LMIN = 2
TILE = 256
STRIP = 16
LOW = 11
HIGH = 6
LEVELS = LOW * HIGH
FIELD = 64
MESH = pl.DeviceIdType.MESH


def transform_matrix(npix, devices):
    top = LMIN + L - 1
    each = -(-L // devices)
    a = [math.comb(2 * k, k) / 4.0**k for k in range(top + 1)]
    product = np.zeros((LEVELS, LEVELS))
    for k in range(LEVELS):
        high, low = divmod(k, LOW)
        product[k, low * HIGH + high] = 1
        if high and low:
            product[k, low * HIGH + high] = 2
            product[k] -= product[high * LOW - low]
    out = np.zeros((devices * each, LEVELS))
    for l in range(LMIN, top + 1):
        owner, place = divmod(l - LMIN, each)
        row = out[owner * each + place]
        for k in range(l + 1):
            row[abs(l - 2 * k)] += a[k] * a[l - k]
        row *= (2 * l + 1) / npix
    return (out @ product).astype(np.float32), each


def pair_up(tiles, n):
    items = []
    for col in range(n):
        mine = sorted((t for t in tiles if t[1] == col), key=lambda t: t[0])
        for k in range(0, len(mine), 2):
            first = mine[k]
            second = mine[k + 1] if k + 1 < len(mine) else (first[0], col, 0)
            items.append((first[0], second[0], first[2], second[2], col))
    return items


def work_tables(n):
    lower = [pair_up([(h * n + i, j, 2) for i in range(n) for j in range(n)], n) for h in range(2)]
    own = [(j, j, 1) for j in range(n)] + [(i, 0, 2) for i in range(1, n)]
    if n % 2:
        own += [(i, j, 2) for j in range(1, n) for i in range(j + 1, n)]
    else:
        own += [
            (1 + (j - 1 + d) % (n - 1), j, 2)
            for j in range(1, n) for d in range(1, n // 2)
        ]
    kinds, needed = [], []
    for h in range(2):
        kinds.append(lower[h])
        needed.append(-1)
    for h in range(2):
        kinds.append(lower[1 - h])
        needed.append(0)
    for h in range(2):
        near = pair_up([(h * n + i, j, w) for i, j, w in own], n)
        far = [
            ((1 - h) * n + i, j, 2)
            for i in range(n) for j in range(n) if (i + j) % 2 == h
        ]
        kinds.append(near + pair_up(far, n))
        needed.append(len(near))
    longest = max(len(k) for k in kinds)
    codes = [
        [row0 + FIELD * (row1 + FIELD * (w0 + FIELD * (w1 + FIELD * col))) for row0, row1, w0, w1, col in k]
        for k in kinds
    ]
    return codes, needed, longest


def spectra_kernel(
    n_rows, n_q, codes, needed, longest, sky_hbm, cov_hbm, cos_hbm, matrix_hbm, weighed, out,
    sky, matrix, cov, x_out, x_in, mine, z_out, z_in, ft, fct, xbuf, buf_a, buf_b, lhs, fj, acc,
    sums, parts, landing, summed, shared,
    in_sem, cov_sem, x_send, x_recv, z_send, z_recv, a_send, a_recv, p_send, p_recv, c_send, c_recv,
    tile_sem, s_send, s_recv, g_send, g_recv, row_ready, all_ready,
):
    r = lax.axis_index("prow")
    c = lax.axis_index("pcol")
    q, h = c // 2, c % 2
    maps = sky.shape[0]
    devices = parts.shape[0]
    each = parts.shape[1]
    me = r * (2 * n_q) + c
    group = maps // n_q
    half = cov.shape[0] // 2
    chunks, width = x_out.shape[0], x_out.shape[2]
    partner = (r, c + 1 - 2 * h)
    diagonal = r == q

    def line(k):
        return lax.rem(q + k, n_q)

    def other(k):
        return lax.rem(r + k, n_rows)

    def placed(j):
        return h * chunks + j

    def cov_copy(j, own):
        side = h if own else 1 - h
        return pltpu.make_async_copy(
            cov_hbm.at[pl.ds(pl.multiple_of(side * half + j * width, width), width)],
            cov.at[pl.ds((int(own) * chunks + j) * width, width)],
            cov_sem.at[int(own) * chunks + j],
        )

    def copy(src, dst, send, recv, device):
        return pltpu.make_async_remote_copy(
            src_ref=src, dst_ref=dst, send_sem=send, recv_sem=recv,
            device_id=device, device_id_type=MESH,
        )

    def x_copy(j):
        return copy(x_out.at[j], x_in.at[j], x_send.at[j], x_recv.at[j], partner)

    def z_copy(j, k):
        return copy(
            z_out.at[j, line(k)], z_in.at[j, k - 1],
            z_send.at[j, k - 1], z_recv.at[j, k - 1], (r, line(k) * 2 + h),
        )

    def a_copy(j, k):
        return copy(
            ft.at[placed(j), q], ft.at[placed(j), q],
            a_send.at[j, k - 1], a_recv.at[j, k - 1], (r, line(k) * 2 + h),
        )

    def a_arrival(j, k):
        g = line(n_q - k)
        return g, copy(
            ft.at[placed(j), g], ft.at[placed(j), g],
            a_send.at[j, k - 1], a_recv.at[j, k - 1], partner,
        )

    def p_copy(j, g, slot):
        return copy(
            ft.at[placed(j), g], ft.at[placed(j), g],
            p_send.at[j, slot], p_recv.at[j, slot], partner,
        )

    def c_copy(j, g, slot, k):
        return copy(
            ft.at[placed(j), g], fct.at[j, g],
            c_send.at[j, slot, k - 1], c_recv.at[j, slot], (other(k), c),
        )

    def product(j, own):
        cov_copy(j, own).wait()
        block = cov[(int(own) * chunks + j) * width : (int(own) * chunks + j + 1) * width, :]
        return lax.dot_general(
            sky[...], block, (((1,), (1,)), ((), ())), preferred_element_type=jnp.float32
        )

    def share(j, g, slot):
        @pl.when(diagonal)
        def _():
            for k in range(1, n_rows):
                c_copy(j, g, slot, k).start()

        p_copy(j, g, slot).start()

    kind = jnp.where(r > q, h, jnp.where(r < q, 2 + h, 4 + h))
    n_strips = 2 * TILE // STRIP

    def by_kind(values):
        chosen = jnp.int32(values[0])
        for i in range(1, len(values)):
            chosen = jnp.where(kind == i, jnp.int32(values[i]), chosen)
        return chosen

    n_items = by_kind([len(k) for k in codes])
    other_from = by_kind(needed)
    item_codes = [by_kind([k[i] if i < len(k) else k[0] for k in codes]) for i in range(longest)]

    def fields(item):
        code = item_codes[0]
        for i in range(1, longest):
            code = jnp.where(item == i, item_codes[i], code)
        found = []
        for _ in range(5):
            found.append(code % FIELD)
            code = code // FIELD
        return found

    def tile_copies(item):
        row0, row1, _, _, col = fields(item)
        for side, row in enumerate((row0, row1)):
            yield pltpu.make_async_copy(
                cos_hbm.at[
                    pl.ds(pl.multiple_of(row * TILE, TILE), TILE),
                    pl.ds(pl.multiple_of(col * TILE, TILE), TILE),
                ],
                xbuf.at[item, pl.ds(side * TILE, TILE)],
                tile_sem.at[item, side],
            )

    def fetch(item, carry):
        for tile in tile_copies(item):
            tile.start()
        return carry

    def landed(item):
        @pl.when(item < n_items)
        def _():
            for tile in tile_copies(item):
                tile.wait()

    def set_operands(item):
        row0, row1, w0, w1, col = fields(item)
        for side, (row, weight) in enumerate(((row0, w0), (row1, w1))):
            value = [ft[row, g].astype(jnp.float32) for g in range(n_q)]
            value = jnp.concatenate(value, axis=0) * weight.astype(jnp.float32)
            lhs[:, side * TILE : (side + 1) * TILE] = value.astype(jnp.bfloat16)
        for g in range(n_q):
            fj[g * group : (g + 1) * group] = fct[col, g].astype(jnp.float32)

    def gen_strip(buf, item, s):
        rows = pl.ds(pl.multiple_of(s * STRIP, STRIP), STRIP)
        x = xbuf[item, rows, :]
        xx = x + x
        buf[1, rows, :] = x.astype(jnp.bfloat16)
        p, t = x, xx * x - 1.0
        for k in range(2, LOW):
            buf[k, rows, :] = t.astype(jnp.bfloat16)
            p, t = t, xx * t - p
        yy = t + t
        buf[LOW, rows, :] = t.astype(jnp.bfloat16)
        p, t = t, yy * t - 1.0
        for k in range(2, HIGH):
            buf[LOW + k - 1, rows, :] = t.astype(jnp.bfloat16)
            p, t = t, yy * t - p

    def item_pass(item, use, gen):
        following = jnp.minimum(item + 1, n_items - 1)
        landed(item + 1)

        @pl.when(item == other_from)
        def _():
            other_half()

        set_operands(item)

        half_tile = TILE // 2
        done = 0
        for level in range(LEVELS):
            k, g = divmod(level, HIGH)
            upto = (level + 1) * n_strips // LEVELS
            for s in range(done, upto):
                gen_strip(gen, following, s)
            done = upto
            if k == 0:
                rhs = use[LOW + g - 1] if g else use[0]
            else:
                rhs = use[LOW + g - 1] * use[k] if g else use[k]
            image = jnp.dot(lhs[...], rhs, preferred_element_type=jnp.float32)
            prod = image * fj[...]
            folded = prod[:, :half_tile] + prod[:, half_tile:]
            acc[level] += folded
            xbuf[longest, 0:8, 0:half_tile] = folded[0:8, :]

    def first_strip(s, carry):
        gen_strip(buf_a, 0, s)
        return carry

    def two_items(pair, carry):
        item_pass(2 * pair, buf_a, buf_b)

        @pl.when(2 * pair + 1 < n_items)
        def _():
            item_pass(2 * pair + 1, buf_b, buf_a)

        return carry

    def member(k):
        device = lax.rem(me + k, devices)
        return (device // (2 * n_q), device % (2 * n_q))

    def each_other(body):
        lax.fori_loop(1, devices, lambda k, carry: (body(k), carry)[1], 0)

    def scatter(k):
        return copy(
            parts.at[lax.rem(me + k, devices)], landing.at[k - 1],
            s_send.at[k - 1], s_recv.at[k - 1], member(k),
        )

    def gather(k, slot):
        return copy(
            summed, shared.at[slot], g_send.at[k - 1], g_recv.at[k - 1], member(k)
        )

    def elsewhere(j, slot):
        g = mirrored(slot)
        where = (1 - h) * chunks + j
        return copy(
            ft.at[where, g], ft.at[where, g],
            p_send.at[j, slot], p_recv.at[j, slot], partner,
        )

    def other_half():
        for j in range(chunks):
            for slot in range(n_q):
                elsewhere(j, slot).wait_recv()

    def mirrored(slot):
        return q if slot == 0 else line(n_q - slot)

    sky_copy = pltpu.make_async_copy(sky_hbm, sky, in_sem.at[0])
    matrix_copy = pltpu.make_async_copy(matrix_hbm, matrix, in_sem.at[1])
    sky_copy.start()
    for own in (False, True):
        for j in range(chunks):
            cov_copy(j, own).start()
    matrix_copy.start()
    lax.fori_loop(0, n_items, fetch, 0)
    barrier = pltpu.get_barrier_semaphore()
    greeted = [partner]
    greeted += [(r, line(k) * 2 + h) for k in range(1, n_q)]
    greeted += [(other(k), c) for k in range(1, n_rows)]
    for device in greeted:
        pl.semaphore_signal(barrier, inc=1, device_id=device, device_id_type=MESH)
    sky_copy.wait()
    for j in range(chunks):
        x_out[j] = product(j, False).astype(x_out.dtype)
        if j == 0:
            pl.semaphore_wait(barrier, len(greeted))
            pl.semaphore_signal(row_ready, inc=1, device_id=partner, device_id_type=MESH)
        x_copy(j).start()
    for j in range(chunks):
        total = product(j, True)
        for g in range(n_q):
            mine[j, g] = total[g * group : (g + 1) * group]
    acc[...] = jnp.zeros_like(acc)
    for buf in (buf_a, buf_b):
        buf[0] = jnp.ones(buf.shape[1:], buf.dtype)
    landed(0)
    lax.fori_loop(0, n_strips, first_strip, 0, unroll=4)
    pl.semaphore_wait(row_ready, 1)
    for k in range(1, n_rows):
        pl.semaphore_signal(all_ready, inc=1, device_id=(other(k), c), device_id_type=MESH)
    for j in range(chunks):
        x_copy(j).wait_recv()
        for g in range(n_q):
            total = mine[j, g] + x_in[j, g * group : (g + 1) * group]
            mine[j, g] = total
            z_out[j, g] = total.astype(z_out.dtype)
        for k in range(1, n_q):
            z_copy(j, k).start()
    lag = min(2, chunks)
    for step in range(chunks + lag):
        if step < chunks:
            j = step
            total = mine[j, q]
            for k in range(1, n_q):
                z_copy(j, k).wait_recv()
                total = total + z_in[j, k - 1]
            ft[placed(j), q] = total.astype(ft.dtype)
            for k in range(1, n_q):
                a_copy(j, k).start()
            share(j, q, 0)
        if step >= lag:
            j = step - lag
            for k in range(1, n_q):
                g, arrival = a_arrival(j, k)
                arrival.wait_recv()
                share(j, g, k)

    @pl.when(diagonal)
    def _():
        for j in range(chunks):
            fct[j] = ft[placed(j)]

    @pl.when(jnp.logical_not(diagonal))
    def _():
        for j in range(chunks):
            for slot in range(n_q):
                copy(
                    ft.at[placed(j), q], fct.at[j, mirrored(slot)],
                    c_send.at[j, slot, 0], c_recv.at[j, slot], partner,
                ).wait_recv()

    lax.fori_loop(0, (n_items + 1) // 2, two_items, 0)
    sums[...] = jnp.zeros_like(sums)
    sums[0:LEVELS, :] = jnp.sum(acc[...], axis=-1)
    matrix_copy.wait()
    spectra = jnp.dot(
        matrix[...], sums[...],
        precision=lax.Precision.HIGHEST, preferred_element_type=jnp.float32,
    )
    for i in range(devices):
        parts[i] = spectra[i * each : (i + 1) * each]
    pl.semaphore_wait(all_ready, n_rows - 1)
    each_other(lambda k: scatter(k).start())

    @pl.when(r > q)
    def _():
        other_half()

    for t in range(2 * chunks):
        for g in range(n_q):
            weighed[g, :, t * width : (t + 1) * width] = ft[t, g]

    @pl.when(diagonal)
    def _():
        for j in range(chunks):
            for slot in range(n_q):
                for k in range(1, n_rows):
                    c_copy(j, mirrored(slot), slot, k).wait_send()

    for j in range(chunks):
        x_copy(j).wait_send()
        for k in range(1, n_q):
            z_copy(j, k).wait_send()
            a_copy(j, k).wait_send()
        for slot in range(n_q):
            p_copy(j, mirrored(slot), slot).wait_send()
    each_other(lambda k: scatter(k).wait_recv())
    summed[...] = lax.fori_loop(0, devices - 1, lambda k, t: t + landing[k], parts[me])
    each_other(lambda k: gather(k, me).start())
    shared[me] = summed[...]
    each_other(lambda k: gather(k, lax.rem(me - k + devices, devices)).wait_recv())
    for i in range(devices):
        if i * each < out.shape[0]:
            out[i * each : (i + 1) * each, :] = shared[i]
    each_other(lambda k: scatter(k).wait_send())
    each_other(lambda k: gather(k, me).wait_send())


def per_device(npix, n_rows, n_cols, inverse_cov, cosines, sky_maps):
    depth, maps = sky_maps.shape
    rows = inverse_cov.shape[0]
    n_q = n_cols // 2
    half, group = rows // 2, maps // n_q
    chunks, width = half // TILE, TILE
    devices = n_rows * n_cols
    codes, needed, longest = work_tables(cosines.shape[1] // TILE)
    matrix, each = transform_matrix(npix, devices)
    padded = -(-LEVELS // 128) * 128
    matrix = np.pad(matrix, ((0, 0), (0, padded - LEVELS)))
    basis = (LOW + HIGH - 1, 2 * TILE, TILE)
    vmem = pl.BlockSpec(memory_space=pltpu.VMEM)
    hbm = pl.BlockSpec(memory_space=pltpu.HBM)
    dma = pltpu.SemaphoreType.DMA
    ft, spectra = pl.pallas_call(
        functools.partial(spectra_kernel, n_rows, n_q, codes, needed, longest),
        out_shape=[
            jax.ShapeDtypeStruct((n_q, group, rows), jnp.bfloat16),
            jax.ShapeDtypeStruct((L, maps), jnp.float32),
        ],
        in_specs=[hbm, hbm, hbm, hbm],
        out_specs=[vmem, vmem],
        scratch_shapes=[
            pltpu.VMEM((maps, depth), jnp.bfloat16),
            pltpu.VMEM(matrix.shape, jnp.float32),
            pltpu.VMEM((rows, depth), jnp.bfloat16),
            pltpu.VMEM((chunks, maps, width), jnp.bfloat16),
            pltpu.VMEM((chunks, maps, width), jnp.bfloat16),
            pltpu.VMEM((chunks, n_q, group, width), jnp.float32),
            pltpu.VMEM((chunks, n_q, group, width), jnp.bfloat16),
            pltpu.VMEM((chunks, n_q - 1, group, width), jnp.bfloat16),
            pltpu.VMEM((2 * chunks, n_q, group, width), jnp.bfloat16),
            pltpu.VMEM((chunks, n_q, group, width), jnp.bfloat16),
            pltpu.VMEM((longest + 1, 2 * TILE, TILE), jnp.float32),
            pltpu.VMEM(basis, jnp.bfloat16),
            pltpu.VMEM(basis, jnp.bfloat16),
            pltpu.VMEM((maps, 2 * TILE), jnp.bfloat16),
            pltpu.VMEM((maps, TILE), jnp.float32),
            pltpu.VMEM((LEVELS, maps, TILE // 2), jnp.float32),
            pltpu.VMEM((padded, maps), jnp.float32),
            pltpu.VMEM((devices, each, maps), jnp.float32),
            pltpu.VMEM((devices - 1, each, maps), jnp.float32),
            pltpu.VMEM((each, maps), jnp.float32),
            pltpu.VMEM((devices, each, maps), jnp.float32),
            dma((2,)), dma((2 * chunks,)),
            dma((chunks,)), dma((chunks,)),
            dma((chunks, n_q - 1)), dma((chunks, n_q - 1)),
            dma((chunks, n_q - 1)), dma((chunks, n_q - 1)),
            dma((chunks, n_q)), dma((chunks, n_q)),
            dma((chunks, n_q, n_rows - 1)), dma((chunks, n_q)),
            dma((longest, 2)),
            dma((devices - 1,)), dma((devices - 1,)),
            dma((devices - 1,)), dma((devices - 1,)),
            pltpu.SemaphoreType.REGULAR, pltpu.SemaphoreType.REGULAR,
        ],
        compiler_params=pltpu.CompilerParams(
            collective_id=1, has_side_effects=True, vmem_limit_bytes=52 * 2**20
        ),
        name="spectra",
    )(sky_maps.T, inverse_cov, cosines, jnp.asarray(matrix))
    return (ft.reshape(maps, rows).T, spectra)


def solution(mesh):
    in_specs = (P("prow", "pcol"), P("prow", "pcol"), P("pcol", None))
    out_specs = (P("prow", None), P())
    n_rows, n_cols = mesh.shape["prow"], mesh.shape["pcol"]

    def whole(inverse_cov, cosines, sky_maps):
        npix = cosines.shape[0]
        step = jax.shard_map(
            functools.partial(per_device, npix, n_rows, n_cols),
            mesh=mesh, in_specs=in_specs, out_specs=out_specs, check_vma=False,
        )
        return step(inverse_cov, cosines, sky_maps)

    return whole
```

time: 96.7 us -> 83.6 us (0.86)
  Pallas kernels: 87.9 us -> 79.5 us
  local copies, waits for them, and re-layouts: 7.57 us -> 3.26 us
    pallas_call x3 -> x1, Pallas kernels: 87.9 us -> 79.5 us  [per_device(): pl.pallas_call(functools.partial(spectra_kernel, n_rows, n_q, codes, need...]
    reshape x2 -> x0, local copies, waits for them, and re-layouts: 2.18 us -> none  [the longest x1 1.51 us: per_device(): spectra = shared.reshape(devices * each, maps)[:L]]
    unnamed x11 -> x6, local copies, waits for them, and re-layouts: 5.39 us -> 3.26 us
where the time goes in v3:
time: 83.6 us; the launch traced here: 83.4 us
  Pallas kernels  79.5 us (95%)
  local copies, waits for them, and re-layouts  3.26 us (4%)
    pallas_call x1, Pallas kernels, per_device(): pl.pallas_call(functools.partial(spectra_kernel, n_rows, n_q, codes, need...  79.5 us
    unnamed x6, local copies, waits for them, and re-layouts  3.26 us

profile of v3, /device:TPU:0, one launch (start us, length us, event | category | flops | bytes accessed | tf_op | source)
XLA Modules:
  0.0 83.4 jit_solution(1523419864540671852)
XLA Ops:
  0.6 0.0 copy-start
  0.6 1.0 %copy-done = bf16[1024,192]{0,1:T(8,128)(2,1)S(1)} copy-done((bf16[1024,192]{0,1:T(8,128)(2,1)S(1)}, bf16[1024,192]{0,1:T(8,128)(2,1)}, u32[]{:S(2)}) %copy-start) | copy-done | bytes 393240
  1.6 0.0 copy-start.1
  1.6 0.8 copy-done.1
  2.4 79.5 %spectra.1 = (bf16[4,48,2048]{2,1,0:T(8,128)(2,1)S(1)}, f32[64,192]{1,0:T(8,128)S(1)}) custom-call(bf16[192,1024]{1,0:T(8,128)(2,1)S(1)} %bitcast.5, bf16[2048,1024]{1,0:T(8,128)(2,1)} %cov_hbm.1, f32[2048,1024]{1,0:T(8,128)} %cos_hbm.1, f32[64,128]{1,0:T(8,128)S(1)} %copy-done.1), custom_call_target="tpu_custom_call" | custom-call | tf_op jit(solution)/shard_map/spectra/pallas_call | solution.py:462
  81.8 0.9 %copy.8 = bf16[2048,192]{0,1:T(8,128)(2,1)} copy(bf16[2048,192]{0,1:T(8,128)(2,1)S(1)} %bitcast.4) | data formatting | bytes 1572864
  82.7 0.6 copy.9
Async XLA Ops:
  0.6 1.0 %copy-start = (bf16[1024,192]{0,1:T(8,128)(2,1)S(1)}, bf16[1024,192]{0,1:T(8,128)(2,1)}, u32[]{:S(2)}) copy-start(bf16[1024,192]{0,1:T(8,128)(2,1)} %param.6) | copy-start | bytes 1179652
  1.6 0.8 copy-start.1

commit v4 on v3

--- a/solution.py
+++ b/solution.py
@@ -17,6 +17,7 @@
 HIGH = 6
 LEVELS = LOW * HIGH
 FIELD = 64
+LAG = 2
 MESH = pl.DeviceIdType.MESH
 
 
@@ -53,7 +54,13 @@
 
 
 def work_tables(n):
-    lower = [pair_up([(h * n + i, j, 2) for i in range(n) for j in range(n)], n) for h in range(2)]
+    lower = [
+        sorted(
+            pair_up([(h * n + i, j, 2) for i in range(n) for j in range(n)], n),
+            key=lambda t: (t[0], t[4]),
+        )
+        for h in range(2)
+    ]
     own = [(j, j, 1) for j in range(n)] + [(i, 0, 2) for i in range(1, n)]
     if n % 2:
         own += [(i, j, 2) for j in range(1, n) for i in range(j + 1, n)]
@@ -70,7 +77,10 @@
         kinds.append(lower[1 - h])
         needed.append(0)
     for h in range(2):
-        near = pair_up([(h * n + i, j, w) for i, j, w in own], n)
+        near = sorted(
+            pair_up([(h * n + i, j, w) for i, j, w in own], n),
+            key=lambda t: max(t[0] - h * n, t[1] - h * n, t[4]),
+        )
         far = [
             ((1 - h) * n + i, j, 2)
             for i in range(n) for j in range(n) if (i + j) % 2 == h
@@ -86,8 +96,8 @@
 
 
 def spectra_kernel(
-    n_rows, n_q, codes, needed, longest, sky_hbm, cov_hbm, cos_hbm, matrix_hbm, weighed, out,
-    sky, matrix, cov, x_out, x_in, mine, z_out, z_in, ft, fct, xbuf, buf_a, buf_b, lhs, fj, acc,
+    n_rows, n_q, codes, needed, longest, sky, cov_hbm, cos_hbm, matrix_hbm, weighed, out,
+    matrix, cov, x_out, x_in, mine, z_out, z_in, ft, fct, xbuf, buf_a, buf_b, lhs, fj, acc,
     sums, parts, landing, summed, shared,
     in_sem, cov_sem, x_send, x_recv, z_send, z_recv, a_send, a_recv, p_send, p_recv, c_send, c_recv,
     tile_sem, s_send, s_recv, g_send, g_recv, row_ready, all_ready,
@@ -177,6 +187,16 @@
 
         p_copy(j, g, slot).start()
 
+    def pass_on(j):
+        for k in range(1, n_q):
+            g, arrival = a_arrival(j, k)
+            arrival.wait_recv()
+            share(j, g, k)
+
+        @pl.when(diagonal)
+        def _():
+            fct[j] = ft[placed(j)]
+
     kind = jnp.where(r > q, h, jnp.where(r < q, 2 + h, 4 + h))
     n_strips = 2 * TILE // STRIP
 
@@ -252,7 +272,26 @@
         following = jnp.minimum(item + 1, n_items - 1)
         landed(item + 1)
 
-        @pl.when(item == other_from)
+        for j in range(max(LAG, chunks - LAG), chunks):
+            @pl.when(item == j - 1)
+            def _():
+                pass_on(j)
+
+        @pl.when(jnp.logical_and(jnp.logical_not(diagonal), item < chunks))
+        def _():
+            for slot in range(n_q):
+                copy(
+                    ft.at[placed(0), q], fct.at[item, mirrored(slot)],
+                    c_send.at[0, slot, 0], c_recv.at[item, slot], partner,
+                ).wait_recv()
+
+        @pl.when(jnp.logical_and(r < q, item % chunks == 0))
+        def _():
+            for i in range(2):
+                for slot in range(n_q):
+                    elsewhere(item // chunks * 2 + i, slot).wait_recv()
+
+        @pl.when(jnp.logical_and(diagonal, item == other_from))
         def _():
             other_half()
 
@@ -274,7 +313,8 @@
             prod = image * fj[...]
             folded = prod[:, :half_tile] + prod[:, half_tile:]
             acc[level] += folded
-            xbuf[longest, 0:8, 0:half_tile] = folded[0:8, :]
+            if (level + 2) * n_strips // LEVELS > upto:
+                xbuf[longest, 0:8, 0:half_tile] = folded[0:8, :]
 
     def first_strip(s, carry):
         gen_strip(buf_a, 0, s)
@@ -323,9 +363,9 @@
     def mirrored(slot):
         return q if slot == 0 else line(n_q - slot)
 
-    sky_copy = pltpu.make_async_copy(sky_hbm, sky, in_sem.at[0])
-    matrix_copy = pltpu.make_async_copy(matrix_hbm, matrix, in_sem.at[1])
-    sky_copy.start()
+    matrix_copy = pltpu.make_async_copy(
+        matrix_hbm.at[pl.ds(0, matrix.shape[0])], matrix, in_sem
+    )
     for own in (False, True):
         for j in range(chunks):
             cov_copy(j, own).start()
@@ -337,7 +377,6 @@
     greeted += [(other(k), c) for k in range(1, n_rows)]
     for device in greeted:
         pl.semaphore_signal(barrier, inc=1, device_id=device, device_id_type=MESH)
-    sky_copy.wait()
     for j in range(chunks):
         x_out[j] = product(j, False).astype(x_out.dtype)
         if j == 0:
@@ -364,39 +403,19 @@
             z_out[j, g] = total.astype(z_out.dtype)
         for k in range(1, n_q):
             z_copy(j, k).start()
-    lag = min(2, chunks)
-    for step in range(chunks + lag):
-        if step < chunks:
-            j = step
-            total = mine[j, q]
-            for k in range(1, n_q):
-                z_copy(j, k).wait_recv()
-                total = total + z_in[j, k - 1]
-            ft[placed(j), q] = total.astype(ft.dtype)
-            for k in range(1, n_q):
-                a_copy(j, k).start()
-            share(j, q, 0)
-        if step >= lag:
-            j = step - lag
-            for k in range(1, n_q):
-                g, arrival = a_arrival(j, k)
-                arrival.wait_recv()
-                share(j, g, k)
-
-    @pl.when(diagonal)
-    def _():
-        for j in range(chunks):
-            fct[j] = ft[placed(j)]
-
-    @pl.when(jnp.logical_not(diagonal))
-    def _():
-        for j in range(chunks):
-            for slot in range(n_q):
-                copy(
-                    ft.at[placed(j), q], fct.at[j, mirrored(slot)],
-                    c_send.at[j, slot, 0], c_recv.at[j, slot], partner,
-                ).wait_recv()
-
+    for j in range(chunks):
+        total = mine[j, q]
+        for k in range(1, n_q):
+            z_copy(j, k).wait_recv()
+            total = total + z_in[j, k - 1]
+        ft[placed(j), q] = total.astype(ft.dtype)
+        for k in range(1, n_q):
+            a_copy(j, k).start()
+        share(j, q, 0)
+        if j >= LAG:
+            pass_on(j - LAG)
+    for j in range(max(chunks - LAG, 0), min(LAG, chunks)):
+        pass_on(j)
     lax.fori_loop(0, (n_items + 1) // 2, two_items, 0)
     sums[...] = jnp.zeros_like(sums)
     sums[0:LEVELS, :] = jnp.sum(acc[...], axis=-1)
@@ -417,7 +436,6 @@
     for t in range(2 * chunks):
         for g in range(n_q):
             weighed[g, :, t * width : (t + 1) * width] = ft[t, g]
-
     @pl.when(diagonal)
     def _():
         for j in range(chunks):
@@ -454,10 +472,10 @@
     codes, needed, longest = work_tables(cosines.shape[1] // TILE)
     matrix, each = transform_matrix(npix, devices)
     padded = -(-LEVELS // 128) * 128
-    matrix = np.pad(matrix, ((0, 0), (0, padded - LEVELS)))
+    matrix = np.pad(matrix, ((0, 4096 - matrix.shape[0]), (0, padded - LEVELS)))
     basis = (LOW + HIGH - 1, 2 * TILE, TILE)
     vmem = pl.BlockSpec(memory_space=pltpu.VMEM)
-    hbm = pl.BlockSpec(memory_space=pltpu.HBM)
+    hbm = pl.BlockSpec(memory_space=pl.ANY)
     dma = pltpu.SemaphoreType.DMA
     ft, spectra = pl.pallas_call(
         functools.partial(spectra_kernel, n_rows, n_q, codes, needed, longest),
@@ -465,11 +483,10 @@
             jax.ShapeDtypeStruct((n_q, group, rows), jnp.bfloat16),
             jax.ShapeDtypeStruct((L, maps), jnp.float32),
         ],
-        in_specs=[hbm, hbm, hbm, hbm],
+        in_specs=[vmem, hbm, hbm, hbm],
         out_specs=[vmem, vmem],
         scratch_shapes=[
-            pltpu.VMEM((maps, depth), jnp.bfloat16),
-            pltpu.VMEM(matrix.shape, jnp.float32),
+            pltpu.VMEM((devices * each, padded), jnp.float32),
             pltpu.VMEM((rows, depth), jnp.bfloat16),
             pltpu.VMEM((chunks, maps, width), jnp.bfloat16),
             pltpu.VMEM((chunks, maps, width), jnp.bfloat16),
@@ -489,7 +506,7 @@
             pltpu.VMEM((devices - 1, each, maps), jnp.float32),
             pltpu.VMEM((each, maps), jnp.float32),
             pltpu.VMEM((devices, each, maps), jnp.float32),
-            dma((2,)), dma((2 * chunks,)),
+            dma, dma((2 * chunks,)),
             dma((chunks,)), dma((chunks,)),
             dma((chunks, n_q - 1)), dma((chunks, n_q - 1)),
             dma((chunks, n_q - 1)), dma((chunks, n_q - 1)),

time: 83.6 us -> 79.4 us (0.950)
  Pallas kernels: 79.5 us -> 76.1 us
    pallas_call x1, Pallas kernels: 79.5 us -> 76.1 us  [per_device(): pl.pallas_call(functools.partial(spectra_kernel, n_rows, n_q, codes, need...]
    unnamed x6 -> x4, local copies, waits for them, and re-layouts: 3.26 us -> 2.5 us
where the time goes in v4:
time: 79.4 us; the launch traced here: 79.3 us
  Pallas kernels  76.1 us (96%)
  local copies, waits for them, and re-layouts  2.5 us (3%)
    pallas_call x1, Pallas kernels, per_device(): pl.pallas_call(functools.partial(spectra_kernel, n_rows, n_q, codes, need...  76.1 us
    unnamed x4, local copies, waits for them, and re-layouts  2.5 us

profile of v4, /device:TPU:0, one launch (start us, length us, event | category | flops | bytes accessed | tf_op | source)
XLA Modules:
  0.0 79.3 jit_solution(10046876133844121323)
XLA Ops:
  0.6 0.0 copy-start
  0.6 1.0 %copy-done = bf16[1024,192]{0,1:T(8,128)(2,1)S(1)} copy-done((bf16[1024,192]{0,1:T(8,128)(2,1)S(1)}, bf16[1024,192]{0,1:T(8,128)(2,1)}, u32[]{:S(2)}) %copy-start) | copy-done | bytes 393240
  1.6 76.1 %spectra.1 = (bf16[4,48,2048]{2,1,0:T(8,128)(2,1)S(1)}, f32[64,192]{1,0:T(8,128)S(1)}) custom-call(bf16[192,1024]{1,0:T(8,128)(2,1)S(1)} %bitcast.5, bf16[2048,1024]{1,0:T(8,128)(2,1)} %cov_hbm.1, f32[2048,1024]{1,0:T(8,128)} %cos_hbm.1, f32[4096,128]{1,0:T(8,128)} %constant.2.clone.matrix_hbm), custom_call_target="tpu_custom_call" | custom-call | tf_op jit(solution)/shard_map/spectra/pallas_call | solution.py:480
  77.8 0.9 %copy.8 = bf16[2048,192]{0,1:T(8,128)(2,1)} copy(bf16[2048,192]{0,1:T(8,128)(2,1)S(1)} %bitcast.4) | data formatting | bytes 1572864
  78.7 0.6 copy.9
Async XLA Ops:
  0.6 1.0 %copy-start = (bf16[1024,192]{0,1:T(8,128)(2,1)S(1)}, bf16[1024,192]{0,1:T(8,128)(2,1)}, u32[]{:S(2)}) copy-start(bf16[1024,192]{0,1:T(8,128)(2,1)} %param.6) | copy-start | bytes 1179652

commit v5 on v4

--- a/solution.py
+++ b/solution.py
@@ -334,7 +334,11 @@
         return (device // (2 * n_q), device % (2 * n_q))
 
     def each_other(body):
-        lax.fori_loop(1, devices, lambda k, carry: (body(k), carry)[1], 0)
+        if devices > 32:
+            lax.fori_loop(1, devices, lambda k, carry: (body(k), carry)[1], 0)
+        else:
+            for k in range(1, devices):
+                body(k)
 
     def scatter(k):
         return copy(

time: 79.4 us -> 79 us (level)
  no operation moved by 1% of the time
where the time goes in v5:
time: 79 us; the launch traced here: 78.8 us
  Pallas kernels  75.7 us (96%)
  local copies, waits for them, and re-layouts  2.5 us (3%)
    pallas_call x1, Pallas kernels, per_device(): pl.pallas_call(functools.partial(spectra_kernel, n_rows, n_q, codes, need...  75.7 us
    unnamed x4, local copies, waits for them, and re-layouts  2.5 us

profile of v5, /device:TPU:0, one launch (start us, length us, event | category | flops | bytes accessed | tf_op | source)
XLA Modules:
  0.0 78.8 jit_solution(12029972514674343578)
XLA Ops:
  0.6 0.0 copy-start
  0.6 1.0 %copy-done = bf16[1024,192]{0,1:T(8,128)(2,1)S(1)} copy-done((bf16[1024,192]{0,1:T(8,128)(2,1)S(1)}, bf16[1024,192]{0,1:T(8,128)(2,1)}, u32[]{:S(2)}) %copy-start) | copy-done | bytes 393240
  1.6 75.7 %spectra.1 = (bf16[4,48,2048]{2,1,0:T(8,128)(2,1)S(1)}, f32[64,192]{1,0:T(8,128)S(1)}) custom-call(bf16[192,1024]{1,0:T(8,128)(2,1)S(1)} %bitcast.5, bf16[2048,1024]{1,0:T(8,128)(2,1)} %cov_hbm.1, f32[2048,1024]{1,0:T(8,128)} %cos_hbm.1, f32[4096,128]{1,0:T(8,128)} %constant.2.clone.matrix_hbm), custom_call_target="tpu_custom_call" | custom-call | tf_op jit(solution)/shard_map/spectra/pallas_call | solution.py:484
  77.3 0.9 %copy.8 = bf16[2048,192]{0,1:T(8,128)(2,1)} copy(bf16[2048,192]{0,1:T(8,128)(2,1)S(1)} %bitcast.4) | data formatting | bytes 1572864
  78.2 0.6 copy.9
Async XLA Ops:
  0.6 1.0 %copy-start = (bf16[1024,192]{0,1:T(8,128)(2,1)S(1)}, bf16[1024,192]{0,1:T(8,128)(2,1)}, u32[]{:S(2)}) copy-start(bf16[1024,192]{0,1:T(8,128)(2,1)} %param.6) | copy-start | bytes 1179652
